TPU v7x, 512 devices: a whole 4x4x16 slice. The times are simulated.
512 devices in a mesh: learner: 16 (over y, x), rollout: 8 (over z_lo), dp: 4 (over z_hi, core).
Axes of the slice: x: 4, y: 4, z: 16 (z_hi: 2, z_lo: 8; z = z_hi * 8 + z_lo), core: 2. Of those that a mesh axis runs over, the one named last changes fastest.
Arguments:
- weight_delta: float32 [8192, 14336], P(('rollout', 'dp'), 'learner'), may hold values from -0.48 to 0.48
- sketch_seed: int32 [1], replicated, may hold values from 0 to 1048575
- up_weight: bfloat16 [8192, 14336], P('rollout', 'learner'), may hold values from -0.0625 to 0.0625
- down_weight: bfloat16 [14336, 8192], P('learner', 'rollout'), may hold values from -0.046875 to 0.046875
- norm_gain: bfloat16 [8192], P('rollout'), may hold values from 0.5 to 1.5
- state_pool: bfloat16 [128, 8192], P(None, 'rollout'), may hold values from -12 to 12
- token_rows: int32 [2, 4, 128], P(None, 'dp'), may hold values from 0 to 127
Outputs:
- decoded: bfloat16 [4, 128, 8192], P('dp', 'learner', 'rollout')
All inputs are finite; a program needn't handle non-finite values.
Results may differ from a plain program's by a relative error of at most 0.017.
Values may be sent and summed in bfloat16 or wider, within the bound.
No kernel may reach another device: no remote copies, remote signals or barrier semaphores. Data moves between devices by JAX's collectives and lax.ppermute only.
A program may use at most 64 MiB of HBM per device.

v0:
```python
import jax
import jax.numpy as jnp
from jax import lax
from jax.sharding import Mesh
from jax.sharding import PartitionSpec as P

D = 8192
RANK = 128
ROLLOUT_DP = ("rollout", "dp_0", "dp_1")
DP = ("dp_0", "dp_1")


epsilon = 1e-05


def sent_to_all(x, axis):
    copies = jnp.broadcast_to(x, (lax.axis_size(axis), *x.shape))
    return lax.all_to_all(copies, axis, split_axis=0, concat_axis=0, tiled=True)


def over_copies(x, axis):
    everything = sent_to_all(x, axis)
    return jnp.sum(everything, axis=0)


def cut_along(x, dim, count):
    dims = x.shape
    parts = x.reshape(*dims[:dim], count, dims[dim] // count, *dims[dim + 1 :])
    return jnp.moveaxis(parts, dim, 0)


def sent_and_summed(x, axis, dim):
    count = lax.axis_size(axis)
    parts = lax.all_to_all(cut_along(x, dim, count), axis, 0, 0, tiled=True)
    return jnp.sum(parts.astype(jnp.float32), axis=0)


def in_order(parts, dim):
    dims = list(parts.shape[1:])
    dims[dim] *= parts.shape[0]
    return jnp.moveaxis(parts, 0, dim).reshape(dims)


def collect(x, axis, dim):
    parts = sent_to_all(x, axis)
    return in_order(parts, dim)


def over_copies_2(x, axis):
    return sent_to_all(x, axis).astype(jnp.float32).sum(axis=0)


def filled_up(lines, count):
    spare = -len(lines) % count
    return jnp.pad(lines, [(0, spare)] + [(0, 0)] * (lines.ndim - 1))


def sum_by_parts(x, axes):
    lines = x.reshape(-1, x.shape[-1])
    padded = filled_up(lines, lax.axis_size(axes))
    whole = collect(sent_and_summed(padded, axes, 0).astype(jnp.bfloat16), axes, 0)
    return lax.slice_in_dim(whole, 0, len(lines)).reshape(x.shape).astype(jnp.float32)


def whole_of(x, axes, dim):
    far, near = axes
    parts = sent_to_all(sent_to_all(x, far), near)
    return in_order(parts.swapaxes(0, 1).reshape(-1, *x.shape), dim)


def sum_in_two_steps(x, axes, dim):
    far, near = axes
    own = sent_and_summed(cut_along(x, dim, lax.axis_size(far)), near, dim + 1)
    return jnp.sum(
        lax.all_to_all(own.astype(jnp.bfloat16), far, 0, 0, tiled=True).astype(jnp.float32), axis=0
    )


def nested_sum(x, axes):
    lines = x.reshape(-1, x.shape[-1])
    padded = filled_up(lines, lax.axis_size(axes[0]) * lax.axis_size(axes[1]))
    whole = whole_of(sum_in_two_steps(padded, axes, 0).astype(jnp.bfloat16), axes, 0)
    return lax.slice_in_dim(whole, 0, len(lines)).reshape(x.shape).astype(jnp.float32)


def sketch(sketch_seed, row_start, row_count, rank_count):
    row_index = row_start + lax.broadcasted_iota(jnp.int32, (row_count, rank_count), 0)
    col_index = lax.broadcasted_iota(jnp.int32, (row_count, rank_count), 1)
    hashed = row_index * rank_count + col_index + sketch_seed[0] * 7919
    hashed = hashed * 1103515245 + 12345
    hashed = hashed ^ lax.shift_right_logical(hashed, jnp.int32(16))
    hashed = hashed * 73244475
    hashed = hashed ^ lax.shift_right_logical(hashed, jnp.int32(15))
    parity = lax.shift_right_logical(hashed, jnp.int32(11)) & 1
    return (2 * parity - 1).astype(jnp.float32)


def apply_layer(inputs, new_weight, down_weight, gain_values):
    values = inputs.astype(jnp.float32)
    square_sum = over_copies(jnp.sum(values * values, axis=1, keepdims=True), "rollout")
    normed = (values * lax.rsqrt(square_sum / D + epsilon) * gain_values).astype(jnp.bfloat16)
    hidden_share = sent_and_summed(
        jnp.dot(normed, new_weight, preferred_element_type=jnp.float32).astype(jnp.bfloat16),
        "rollout",
        0,
    )
    hidden = jax.nn.silu(hidden_share).astype(jnp.bfloat16)
    return jnp.dot(collect(hidden, "rollout", 0), down_weight, preferred_element_type=jnp.float32)


def local(weight_delta, sketch_seed, up_weight, down_weight, norm_gain, state_pool, token_rows):
    precise = lax.Precision.HIGHEST
    local_cols = weight_delta.shape[1]
    sketch_matrix = sketch(sketch_seed, lax.axis_index("learner") * local_cols, local_cols, RANK)
    partial_range = jnp.dot(
        weight_delta, sketch_matrix, precision=precise, preferred_element_type=jnp.float32
    )
    range_basis = over_copies_2(partial_range.astype(jnp.bfloat16), "learner").astype(jnp.float32)
    partial_gram = jnp.dot(
        range_basis.T, range_basis, precision=precise, preferred_element_type=jnp.float32
    )
    gram_matrix = sum_by_parts(partial_gram.astype(jnp.bfloat16), ROLLOUT_DP)
    lower_factor = jnp.linalg.cholesky(gram_matrix)
    ortho_basis = lax.linalg.triangular_solve(
        lower_factor, range_basis, left_side=False, lower=True, transpose_a=True
    )
    partial_coef = jnp.dot(
        ortho_basis.T, weight_delta, precision=precise, preferred_element_type=jnp.float32
    )
    coefficients = nested_sum(partial_coef.astype(jnp.bfloat16), (("rollout", "dp_0"), "dp_1"))
    basis_block = collect(ortho_basis.astype(jnp.bfloat16), DP, 0).astype(ortho_basis.dtype)
    update = jnp.dot(
        basis_block, coefficients, precision=precise, preferred_element_type=jnp.float32
    )
    new_weight = (up_weight.astype(jnp.float32) + update).astype(jnp.bfloat16)
    gain_values = norm_gain.astype(jnp.float32)
    picked = token_rows[:, 0, :]
    first_rows = state_pool[picked[0]]
    partial_one = apply_layer(first_rows, new_weight, down_weight, gain_values)
    step_one = sum_by_parts(partial_one.astype(jnp.bfloat16), "learner")
    carried = (first_rows.astype(jnp.float32) + step_one).astype(jnp.bfloat16)
    second_rows = (carried.astype(jnp.float32) + state_pool[picked[1]].astype(jnp.float32)).astype(
        jnp.bfloat16
    )
    partial_two = apply_layer(second_rows, new_weight, down_weight, gain_values)
    last_share = sent_and_summed(partial_two.astype(jnp.bfloat16), "learner", 0)
    share_rows = last_share.shape[0]
    own_rows = lax.dynamic_slice_in_dim(
        second_rows, lax.axis_index("learner") * share_rows, share_rows, 0
    )
    return (own_rows.astype(jnp.float32) + last_share).astype(jnp.bfloat16)[None]


def solution(mesh):
    torus = Mesh(
        mesh.devices.reshape(mesh.shape["learner"], mesh.shape["rollout"], 2, 2),
        ("learner", "rollout", "dp_0", "dp_1"),
    )
    return jax.shard_map(
        local,
        mesh=torus,
        in_specs=(
            P(ROLLOUT_DP, "learner"),
            P(),
            P("rollout", "learner"),
            P("learner", "rollout"),
            P("rollout"),
            P(None, "rollout"),
            P(None, DP, None),
        ),
        out_specs=P(DP, "learner", "rollout"),
        check_vma=False,
    )
```

profile of v0, /device:TPU:2, one launch (start us, length us, event | category | flops | bytes accessed | tf_op | source)
XLA Modules:
  0.0 319.2 jit_solution(2642349887146297860)
XLA Ops:
  0.8 2.5 fusion.2
  3.6 23.3 %all_to_all.85 = bf16[16,256,128]{2,1,0:T(8,128)(2,1)S(1)} all-to-all(bf16[16,256,128]{2,1,0:T(8,128)(2,1)S(1)} %broadcast_in_dim.42), channel_id=1, replica_groups=mesh['learner'=16,'rollout'=8,'dp_0'=2,'dp_1'=2] {'learner'}, dimensions={0} | all-to-all | bytes 2097152 | tf_op jit(solution)/shard_map/all_to_all | solution.py:18
  27.4 27.4 %all_to_all.86 = bf16[32,4,128]{2,1,0:T(4,128)(2,1)S(1)} all-to-all(bf16[32,4,128]{2,1,0:T(4,128)(2,1)S(1)} %bitcast.87), channel_id=1, replica_groups=mesh['learner'=16,'rollout'=8,'dp_0'=2,'dp_1'=2] {'rollout','dp_0','dp_1'}, dimensions={0} | all-to-all | bytes 65536 | tf_op jit(solution)/shard_map/all_to_all | solution.py:34
  54.9 15.1 %all_to_all.87 = bf16[32,4,128]{2,1,0:T(4,128)(2,1)S(1)} all-to-all(bf16[32,4,128]{2,1,0:T(4,128)(2,1)S(1)} %broadcast_in_dim.43), channel_id=1, replica_groups=mesh['learner'=16,'rollout'=8,'dp_0'=2,'dp_1'=2] {'rollout','dp_0','dp_1'}, dimensions={0} | all-to-all | bytes 65536 | tf_op jit(solution)/shard_map/all_to_all | solution.py:18
  70.2 11.7 %cholesky.16 = f32[128,128]{1,0:T(8,128)S(1)} custom-call(f32[128,128]{1,0:T(8,128)S(1)} %fusion.42), custom_call_target="Cholesky" | custom-call | tf_op jit(solution)/shard_map/jit(cholesky)/cholesky | solution.py:123
  83.2 9.8 %custom-call.6 = f32[1,128,128]{1,2,0:T(8,128)S(1)} custom-call(f32[1,128,128]{2,1,0:T(8,128)S(1)} %fusion.39), custom_call_target="InvertDiagBlocksLowerTriangular" | custom-call | tf_op jit(solution)/shard_map/triangular_solve | solution.py:124
  94.2 3.9 %all_to_all.88 = bf16[2,16,4,896]{3,2,1,0:T(4,128)(2,1)S(1)} all-to-all(bf16[2,16,4,896]{3,2,1,0:T(4,128)(2,1)S(1)} %bitcast.84), channel_id=1, replica_groups=mesh['learner'=16,'rollout'=8,'dp_0'=2,'dp_1'=2] {'dp_1'}, dimensions={0} | all-to-all | bytes 458752 | tf_op jit(solution)/shard_map/all_to_all | solution.py:34
  98.1 0.8 reduce_sum.126
  98.9 3.5 %all-to-all-start.6 = ((bf16[16,4,896]{2,1,0:T(4,128)(2,1)}), bf16[16,4,896]{2,1,0:T(4,128)(2,1)S(1)}, u32[]{:S(2)}, u32[]{:S(2)}) async-start(bf16[16,4,896]{2,1,0:T(4,128)(2,1)} %reduce_sum.126), calls=%async_computation.6 | async-start | bytes 229376 | tf_op jit(solution)/shard_map/all_to_all | solution.py:75
  102.5 0.9 gather_fusion
  103.5 13.7 %all-to-all-done.6 = bf16[16,4,896]{2,1,0:T(4,128)(2,1)S(1)} async-done(((bf16[16,4,896]{2,1,0:T(4,128)(2,1)}), bf16[16,4,896]{2,1,0:T(4,128)(2,1)S(1)}, u32[]{:S(2)}, u32[]{:S(2)}) %all-to-all-start.6) | async-done | bytes 114720 | tf_op jit(solution)/shard_map/all_to_all | solution.py:75
  117.7 3.5 %all-to-all-start = ((f32[8,128,1]{1,2,0:T(1,128)}), f32[8,128,1]{1,2,0:T(1,128)S(1)}, u32[]{:S(2)}, u32[]{:S(2)}) async-start(f32[8,128,1]{1,2,0:T(1,128)} %broadcast_in_dim.41), calls=%async_computation | async-start | bytes 8192 | tf_op jit(solution)/shard_map/all_to_all | solution.py:18
  121.3 10.3 %all-to-all-done = f32[8,128,1]{1,2,0:T(1,128)S(1)} async-done(((f32[8,128,1]{1,2,0:T(1,128)}), f32[8,128,1]{1,2,0:T(1,128)S(1)}, u32[]{:S(2)}, u32[]{:S(2)}) %all-to-all-start) | async-done | bytes 4128 | tf_op jit(solution)/shard_map/all_to_all | solution.py:18
  131.6 22.3 %all_to_all.89 = bf16[16,4,896]{2,1,0:T(4,128)(2,1)S(1)} all-to-all(bf16[16,4,896]{2,1,0:T(4,128)(2,1)S(1)} %broadcast_in_dim.45), channel_id=1, replica_groups=mesh['learner'=16,'rollout'=8,'dp_0'=2,'dp_1'=2] {'rollout','dp_0'}, dimensions={0} | all-to-all | bytes 229376 | tf_op jit(solution)/shard_map/all_to_all | solution.py:18
  154.0 3.9 %all_to_all.90 = bf16[2,16,4,896]{3,2,1,0:T(4,128)(2,1)S(1)} all-to-all(bf16[2,16,4,896]{3,2,1,0:T(4,128)(2,1)S(1)} %broadcast_in_dim.46), channel_id=1, replica_groups=mesh['learner'=16,'rollout'=8,'dp_0'=2,'dp_1'=2] {'dp_1'}, dimensions={0} | all-to-all | bytes 458752 | tf_op jit(solution)/shard_map/all_to_all | solution.py:18
  158.6 3.6 %all-to-all-start.4 = ((bf16[4,256,128]{2,1,0:T(8,128)(2,1)}), bf16[4,256,128]{2,1,0:T(8,128)(2,1)S(1)}, u32[]{:S(2)}, u32[]{:S(2)}) async-start(bf16[4,256,128]{2,1,0:T(8,128)(2,1)} %broadcast_in_dim.44), calls=%async_computation.4 | async-start | bytes 524288 | tf_op jit(solution)/shard_map/all_to_all | solution.py:18
  162.4 14.6 %all-to-all-done.4 = bf16[4,256,128]{2,1,0:T(8,128)(2,1)S(1)} async-done(((bf16[4,256,128]{2,1,0:T(8,128)(2,1)}), bf16[4,256,128]{2,1,0:T(8,128)(2,1)S(1)}, u32[]{:S(2)}, u32[]{:S(2)}) %all-to-all-start.4) | async-done | bytes 262176 | tf_op jit(solution)/shard_map/all_to_all | solution.py:18
  177.0 2.1 add_convert_fusion
  179.7 31.0 %all_to_all.91 = bf16[8,16,896]{2,1,0:T(8,128)(2,1)S(1)} all-to-all(bf16[8,16,896]{2,1,0:T(8,128)(2,1)S(1)} %bitcast.80), channel_id=1, replica_groups=mesh['learner'=16,'rollout'=8,'dp_0'=2,'dp_1'=2] {'rollout'}, dimensions={0} | all-to-all | bytes 458752 | tf_op jit(solution)/shard_map/all_to_all | solution.py:34
  210.7 19.2 %all_to_all.92 = bf16[8,16,896]{2,1,0:T(8,128)(2,1)S(1)} all-to-all(bf16[8,16,896]{2,1,0:T(8,128)(2,1)S(1)} %broadcast_in_dim.47), channel_id=1, replica_groups=mesh['learner'=16,'rollout'=8,'dp_0'=2,'dp_1'=2] {'rollout'}, dimensions={0} | all-to-all | bytes 458752 | tf_op jit(solution)/shard_map/all_to_all | solution.py:18
  230.4 11.6 %all_to_all.93 = bf16[16,8,1024]{2,1,0:T(8,128)(2,1)S(1)} all-to-all(bf16[16,8,1024]{2,1,0:T(8,128)(2,1)S(1)} %fusion), channel_id=1, replica_groups=mesh['learner'=16,'rollout'=8,'dp_0'=2,'dp_1'=2] {'learner'}, dimensions={0} | all-to-all | bytes 524288 | tf_op jit(solution)/shard_map/all_to_all | solution.py:34
  242.8 4.8 %all-to-all-start.12 = ((bf16[16,8,1024]{2,1,0:T(8,128)(2,1)}), bf16[16,8,1024]{2,1,0:T(8,128)(2,1)S(1)}, u32[]{:S(2)}, u32[]{:S(2)}) async-start(bf16[16,8,1024]{2,1,0:T(8,128)(2,1)} %broadcast_in_dim.48), calls=%async_computation.12 | async-start | bytes 524288 | tf_op jit(solution)/shard_map/all_to_all | solution.py:18
  247.6 0.9 gather_fusion.1
  248.5 6.5 %all-to-all-done.12 = bf16[16,8,1024]{2,1,0:T(8,128)(2,1)S(1)} async-done(((bf16[16,8,1024]{2,1,0:T(8,128)(2,1)}), bf16[16,8,1024]{2,1,0:T(8,128)(2,1)S(1)}, u32[]{:S(2)}, u32[]{:S(2)}) %all-to-all-start.12) | async-done | bytes 262176 | tf_op jit(solution)/shard_map/all_to_all | solution.py:18
  255.9 5.5 %all-to-all-start.13 = ((f32[8,128,1]{1,2,0:T(1,128)}), f32[8,128,1]{1,2,0:T(1,128)S(1)}, u32[]{:S(2)}, u32[]{:S(2)}) async-start(f32[8,128,1]{1,2,0:T(1,128)} %broadcast_in_dim.49), calls=%async_computation.13 | async-start | bytes 8192 | tf_op jit(solution)/shard_map/all_to_all | solution.py:18
  261.5 10.2 %all-to-all-done.13 = f32[8,128,1]{1,2,0:T(1,128)S(1)} async-done(((f32[8,128,1]{1,2,0:T(1,128)}), f32[8,128,1]{1,2,0:T(1,128)S(1)}, u32[]{:S(2)}, u32[]{:S(2)}) %all-to-all-start.13) | async-done | bytes 4128 | tf_op jit(solution)/shard_map/all_to_all | solution.py:18
  271.8 2.0 convolution_convert_fusion.2
  273.8 14.8 %all_to_all.94 = bf16[8,16,896]{2,1,0:T(8,128)(2,1)S(1)} all-to-all(bf16[8,16,896]{2,1,0:T(8,128)(2,1)S(1)} %bitcast.79), channel_id=1, replica_groups=mesh['learner'=16,'rollout'=8,'dp_0'=2,'dp_1'=2] {'rollout'}, dimensions={0} | all-to-all | bytes 458752 | tf_op jit(solution)/shard_map/all_to_all | solution.py:34
  288.6 16.6 %all_to_all.95 = bf16[8,16,896]{2,1,0:T(8,128)(2,1)S(1)} all-to-all(bf16[8,16,896]{2,1,0:T(8,128)(2,1)S(1)} %broadcast_in_dim.50), channel_id=1, replica_groups=mesh['learner'=16,'rollout'=8,'dp_0'=2,'dp_1'=2] {'rollout'}, dimensions={0} | all-to-all | bytes 458752 | tf_op jit(solution)/shard_map/all_to_all | solution.py:18
  305.2 1.1 fusion.1
  306.4 4.8 %all-to-all-start.16 = ((bf16[16,8,1024]{2,1,0:T(8,128)(2,1)}), bf16[16,8,1024]{2,1,0:T(8,128)(2,1)S(1)}, u32[]{:S(2)}, u32[]{:S(2)}) async-start(bf16[16,8,1024]{2,1,0:T(8,128)(2,1)} %fusion.1), calls=%async_computation.16 | async-start | bytes 524288 | tf_op jit(solution)/shard_map/all_to_all | solution.py:34
  311.2 7.4 %all-to-all-done.16 = bf16[16,8,1024]{2,1,0:T(8,128)(2,1)S(1)} async-done(((bf16[16,8,1024]{2,1,0:T(8,128)(2,1)}), bf16[16,8,1024]{2,1,0:T(8,128)(2,1)S(1)}, u32[]{:S(2)}, u32[]{:S(2)}) %all-to-all-start.16) | async-done | bytes 262176 | tf_op jit(solution)/shard_map/all_to_all | solution.py:34
  (60 shorter events, 8.9 us)
Async XLA Ops:
  0.0 229.9 %copy-start = (bf16[896,1024]{1,0:T(8,128)(2,1)S(1)}, bf16[896,1024]{1,0:T(8,128)(2,1)}, u32[]{:S(2)}) copy-start(bf16[896,1024]{1,0:T(8,128)(2,1)} %param.10) | copy-start | bytes 5505028
  3.6 89.7 %copy-start.3 = (f32[256,896]{1,0:T(8,128)S(1)}, f32[256,896]{1,0:T(8,128)}, u32[]{:S(2)}) copy-start(f32[256,896]{1,0:T(8,128)} %param.7) | copy-start | bytes 2752516
  83.2 19.2 %copy-start.5 = (s32[2,1,128]{2,1,0:T(1,128)S(1)}, s32[2,1,128]{2,1,0:T(1,128)}, u32[]{:S(2)}) copy-start(s32[2,1,128]{2,1,0:T(1,128)} %param.13) | copy-start | bytes 3076
  83.2 19.2 %copy-start.1 = (bf16[128,1024]{1,0:T(8,128)(2,1)S(1)}, bf16[128,1024]{1,0:T(8,128)(2,1)}, u32[]{:S(2)}) copy-start(bf16[128,1024]{1,0:T(8,128)(2,1)} %param.12) | copy-start | bytes 786436
  98.9 18.2 %all-to-all-start.6 = ((bf16[16,4,896]{2,1,0:T(4,128)(2,1)}), bf16[16,4,896]{2,1,0:T(4,128)(2,1)S(1)}, u32[]{:S(2)}, u32[]{:S(2)}) async-start(bf16[16,4,896]{2,1,0:T(4,128)(2,1)} %reduce_sum.126), calls=%async_computation.6 | async-start | bytes 229376 | tf_op jit(solution)/shard_map/all_to_all | solution.py:75
  102.5 59.7 %copy-start.4 = (bf16[1024]{0:T(1024)(128)(2,1)S(1)}, bf16[1024]{0:T(1024)(128)(2,1)}, u32[]{:S(2)}) copy-start(bf16[1024]{0:T(1024)(128)(2,1)} %param.11) | copy-start | bytes 6148
  117.7 13.8 %all-to-all-start = ((f32[8,128,1]{1,2,0:T(1,128)}), f32[8,128,1]{1,2,0:T(1,128)S(1)}, u32[]{:S(2)}, u32[]{:S(2)}) async-start(f32[8,128,1]{1,2,0:T(1,128)} %broadcast_in_dim.41), calls=%async_computation | async-start | bytes 8192 | tf_op jit(solution)/shard_map/all_to_all | solution.py:18
  158.6 18.4 %all-to-all-start.4 = ((bf16[4,256,128]{2,1,0:T(8,128)(2,1)}), bf16[4,256,128]{2,1,0:T(8,128)(2,1)S(1)}, u32[]{:S(2)}, u32[]{:S(2)}) async-start(bf16[4,256,128]{2,1,0:T(8,128)(2,1)} %broadcast_in_dim.44), calls=%async_computation.4 | async-start | bytes 524288 | tf_op jit(solution)/shard_map/all_to_all | solution.py:18
  179.1 50.8 %copy-start.2 = (bf16[1024,896]{1,0:T(8,128)(2,1)}, bf16[1024,896]{1,0:T(8,128)(2,1)S(1)}, u32[]{:S(2)}) copy-start(bf16[1024,896]{1,0:T(8,128)(2,1)S(1)} %add_convert_fusion) | copy-start | bytes 5505028
  242.8 12.2 %all-to-all-start.12 = ((bf16[16,8,1024]{2,1,0:T(8,128)(2,1)}), bf16[16,8,1024]{2,1,0:T(8,128)(2,1)S(1)}, u32[]{:S(2)}, u32[]{:S(2)}) async-start(bf16[16,8,1024]{2,1,0:T(8,128)(2,1)} %broadcast_in_dim.48), calls=%async_computation.12 | async-start | bytes 524288 | tf_op jit(solution)/shard_map/all_to_all | solution.py:18
  255.9 15.8 %all-to-all-start.13 = ((f32[8,128,1]{1,2,0:T(1,128)}), f32[8,128,1]{1,2,0:T(1,128)S(1)}, u32[]{:S(2)}, u32[]{:S(2)}) async-start(f32[8,128,1]{1,2,0:T(1,128)} %broadcast_in_dim.49), calls=%async_computation.13 | async-start | bytes 8192 | tf_op jit(solution)/shard_map/all_to_all | solution.py:18
  306.4 12.2 %all-to-all-start.16 = ((bf16[16,8,1024]{2,1,0:T(8,128)(2,1)}), bf16[16,8,1024]{2,1,0:T(8,128)(2,1)S(1)}, u32[]{:S(2)}, u32[]{:S(2)}) async-start(bf16[16,8,1024]{2,1,0:T(8,128)(2,1)} %fusion.1), calls=%async_computation.16 | async-start | bytes 524288 | tf_op jit(solution)/shard_map/all_to_all | solution.py:34
where the time goes:
time: 320 us; the launch traced here: 319 us
  blocking collectives  189 us (59%)
  waiting for transfers between devices  62.7 us (20%)
  starting transfers between devices  25.6 us (8%)
  other arithmetic  25.3 us (8%)
  matrix products  9.98 us (3%)
  local copies, waits for them, and re-layouts  5.34 us (2%)
    all_to_all x6, blocking collectives, sent_to_all(): return lax.all_to_all(copies, axis, split_axis=0, concat_axis=0, tiled=True)  100 us
    all_to_all x5, blocking collectives, sent_and_summed(): parts = lax.all_to_all(cut_along(x, dim, count), axis, 0, 0, tiled=True)  88.7 us
    all_to_all x4, waiting for transfers between devices, sent_to_all(): return lax.all_to_all(copies, axis, split_axis=0, concat_axis=0, tiled=True)  41.6 us
    all_to_all x4, starting transfers between devices, sent_to_all(): return lax.all_to_all(copies, axis, split_axis=0, concat_axis=0, tiled=True)  17.4 us
    all_to_all x1, waiting for transfers between devices, sum_in_two_steps(): lax.all_to_all(own.astype(jnp.bfloat16), far, 0, 0, tiled=True)  13.7 us
    another operation x3, other arithmetic, local(): lower_factor = jnp.linalg.cholesky(gram_matrix)  12.4 us
    another operation x2, other arithmetic, local(): lax.linalg.triangular_solve(lower_factor, range_basis, left_side=False, l...  10.5 us
    all_to_all x1, waiting for transfers between devices, sent_and_summed(): parts = lax.all_to_all(cut_along(x, dim, count), axis, 0, 0, tiled=True)  7.42 us
  transfers between devices with their start and end apart: 6, of which 6 were waited for; matrix products, arithmetic and copies ran while one was open for 1% of the time, Pallas kernels for 0%

commit v1 on v0

v1 whole, which is shorter than its diff:
```python
import functools

import jax
import jax.numpy as jnp
from jax import lax
from jax.experimental import pallas as pl
from jax.experimental.pallas import tpu as pltpu
from jax.sharding import Mesh
from jax.sharding import PartitionSpec as P

D = 8192
RANK = 128
EPS = 1e-05
L = ("y", "x")
CL = ("c", "y", "x")
Z = ("zl", "zh")
BF = jnp.bfloat16
F32 = jnp.float32


def swap(x, axis):
    return lax.all_to_all(x, axis, split_axis=0, concat_axis=0, tiled=True)


def sent_to_all(x, axis):
    return swap(jnp.broadcast_to(x, (lax.axis_size(axis), *x.shape)), axis)


def summed(x, axis):
    count = lax.axis_size(axis)
    parts = swap(x.reshape(count, x.shape[0] // count, x.shape[1]), axis)
    return jnp.sum(parts.astype(F32), axis=0)


def dot(a, b):
    return jnp.dot(a, b, preferred_element_type=F32)


def dot_t(a, b):
    return lax.dot_general(a, b, (((0,), (0,)), ((), ())), preferred_element_type=F32)


def sketch(sketch_seed, row_start, row_count, rank_count):
    row_index = row_start + lax.broadcasted_iota(jnp.int32, (row_count, rank_count), 0)
    col_index = lax.broadcasted_iota(jnp.int32, (row_count, rank_count), 1)
    hashed = row_index * rank_count + col_index + sketch_seed[0] * 7919
    hashed = hashed * 1103515245 + 12345
    hashed = hashed ^ lax.shift_right_logical(hashed, jnp.int32(16))
    hashed = hashed * 73244475
    hashed = hashed ^ lax.shift_right_logical(hashed, jnp.int32(15))
    parity = lax.shift_right_logical(hashed, jnp.int32(11)) & 1
    return (2 * parity - 1).astype(F32)


def hi_lo(x):
    hi = lax.reduce_precision(x, 8, 7)
    return hi, x - hi


def diagonal_offset(rows, first):
    row = first + lax.broadcasted_iota(jnp.int32, (rows, RANK), 0)
    col = lax.broadcasted_iota(jnp.int32, (rows, RANK), 1)
    return (col - row) & (RANK - 1)


def precise(a, b):
    return jnp.dot(a, b, precision=lax.Precision.HIGHEST, preferred_element_type=F32)


def first_hidden_kernel(half, z_ref, hidden_ref, coef_ref, pre_ref):
    packed = z_ref[:, 2 * half : 2 * half + RANK].astype(F32)
    row = lax.broadcasted_iota(jnp.int32, (RANK, RANK), 0)
    col = lax.broadcasted_iota(jnp.int32, (RANK, RANK), 1)
    offset = (col - row) & (RANK - 1)
    squares = jnp.sum(jnp.where(offset >= RANK - 2, packed, 0.0), axis=1, keepdims=True)
    gram = jnp.where(offset <= RANK // 2, packed, packed.T)
    eye = jnp.where(row == col, 1.0, 0.0)
    on_diag = gram * eye
    scale_col = lax.rsqrt(jnp.sum(on_diag, axis=1, keepdims=True))
    scale_row = lax.rsqrt(jnp.sum(on_diag, axis=0, keepdims=True))
    unit = gram * scale_col * scale_row
    bound = jnp.max(jnp.sum(jnp.abs(unit), axis=1, keepdims=True), axis=0, keepdims=True)
    step = 2.0 / (1.0 + bound)
    start = step * (2.0 * eye - step * unit)

    def going(state):
        count, error, _ = state
        return jnp.logical_and(count < 40, error > 1e-5)

    def refine(state):
        count, _, inverse = state
        left = eye - precise(unit, inverse)
        return count + 1, jnp.sum(left * left), inverse + precise(inverse, left)

    _, _, inverse = lax.while_loop(going, refine, (0, jnp.float32(1.0), start))
    moved = z_ref[:, :half].astype(F32) * scale_col
    coef = (precise(inverse, moved) * scale_col).astype(BF)
    coef_ref[...] = coef
    total = z_ref[:, half : 2 * half].astype(F32) + jnp.dot(
        z_ref[:, 2 * half + RANK :], coef, preferred_element_type=F32
    )
    pre_ref[...] = total.astype(BF)
    pre = total * lax.rsqrt(squares / D + EPS)
    hidden_ref[...] = (pre / (1.0 + jnp.exp(-pre))).astype(BF)


def first_hidden(gathered, half):
    shape = jax.ShapeDtypeStruct((RANK, half), BF)
    return pl.pallas_call(
        functools.partial(first_hidden_kernel, half),
        out_shape=(shape, shape, shape),
        in_specs=[pl.BlockSpec(memory_space=pltpu.VMEM)],
        out_specs=(pl.BlockSpec(memory_space=pltpu.VMEM),) * 3,
    )(gathered)


def local(weight_delta, sketch_seed, up_weight, down_weight, norm_gain, state_pool, token_rows):
    core = lax.axis_index("c")
    z_half = lax.axis_index("zh")
    z_own = lax.axis_index(Z)
    learner = lax.axis_index(L)
    rows, cols = weight_delta.shape
    half = cols // 2
    width = 2 * rows
    pool_rows = state_pool.shape[0]

    def own_half(x):
        return jnp.where(core == 0, x[:, :half], x[:, half:])

    tokens = token_rows[:, 0, :].reshape(-1, 1)
    delta = weight_delta.astype(BF)
    kept = own_half(delta)
    other = jnp.where(core == 0, delta[:, half:], delta[:, :half])
    sent = jnp.concatenate([other, tokens.astype(BF)], axis=1)
    received = lax.ppermute(sent, "c", [(0, 1), (1, 0)])

    signs = sketch(sketch_seed, learner * cols, cols, RANK).astype(BF)
    range_share = summed(dot(delta, signs).astype(BF), L).astype(BF)
    basis = sent_to_all(range_share, CL).reshape(width, RANK)

    basis_own = lax.dynamic_slice_in_dim(basis, core * rows, rows, 0)
    basis_other = lax.dynamic_slice_in_dim(basis, (1 - core) * rows, rows, 0)
    other_tokens = received[:, half:].astype(jnp.int32)

    pool_half = lax.dynamic_slice_in_dim(state_pool, z_half * width, width, 1)
    gain_half = lax.dynamic_slice_in_dim(norm_gain, z_half * width, width, 0).astype(F32)
    up_half = lax.dynamic_slice_in_dim(up_weight, z_half * width, width, 0)
    down_half = lax.dynamic_slice_in_dim(down_weight, core * half, half, 0)

    pool_wide = pool_half.astype(F32)
    pool_gained = (pool_wide * gain_half).astype(BF)
    squares = jnp.sum(pool_wide * pool_wide, axis=1, keepdims=True)

    moved = dot_t(basis_own, kept) + dot_t(basis_other, received[:, :half])
    pool_up = own_half(dot(pool_gained, up_half))
    offset = diagonal_offset(RANK, 0)
    hi, lo = hi_lo(squares)

    def packed(gram, hi, lo, offset):
        rest = jnp.where(offset == RANK - 1, lo, jnp.where(offset == RANK - 2, hi, 0.0))
        return jnp.where(offset <= RANK // 2, gram, rest)

    gram = packed(dot_t(basis, basis), hi, lo, offset)
    pool_basis = dot(pool_gained, basis)
    stacked = jnp.concatenate([moved, pool_up, gram, pool_basis], axis=1).astype(BF)
    share = summed(stacked, Z)
    share_rows = share.shape[0]
    offset = diagonal_offset(share_rows, z_own * share_rows)
    gram = share[:, 2 * half : 2 * half + RANK]
    hi, lo = hi_lo(jnp.sum(jnp.where(offset >= RANK - 2, gram, 0.0), axis=1, keepdims=True))
    gram = packed(gram, hi, lo, offset)
    share = jnp.concatenate(
        [share[:, : 2 * half], gram, share[:, 2 * half + RANK :]], axis=1
    ).astype(BF)
    gathered = sent_to_all(share, Z).reshape(RANK, -1)

    hidden, coef, pool_pre = first_hidden(gathered, half)
    step_share = summed(dot(hidden, down_half).astype(BF), CL).astype(BF)
    step_one = sent_to_all(step_share, CL).reshape(pool_rows, -1)
    carried = (state_pool.astype(F32) + step_one.astype(F32)).astype(BF)
    carried_half = lax.dynamic_slice_in_dim(carried, z_half * width, width, 1)
    carried_gained = (carried_half.astype(F32) * gain_half).astype(BF)

    up_share = own_half(dot(carried_gained, up_half)) + dot(
        dot(carried_gained, basis).astype(BF), coef
    )

    first_core = jnp.where(core == 0, tokens, other_tokens)
    last_core = jnp.where(core == 0, other_tokens, tokens)
    count = pool_rows
    choice = lax.broadcasted_iota(jnp.int32, (2 * count, pool_rows), 1)

    def picks(step):
        span = slice(step * count, (step + 1) * count)
        both = jnp.concatenate([first_core[span], last_core[span]], axis=0)
        return (both == choice).astype(BF)

    pick_one, pick_two = picks(0), picks(1)
    second = (dot(pick_one, carried) + dot(pick_two, state_pool)).astype(BF).astype(F32)
    squares = jnp.sum(second * second, axis=1, keepdims=True)
    tail = jnp.concatenate([squares[:count], squares[count:]], axis=1)
    tail = jnp.concatenate(
        [jnp.where(z_half == 0, tail, 0.0), jnp.where(z_half == 1, tail, 0.0)], axis=1
    )
    blank = jnp.zeros((count, 4 * RANK - half - 8), F32)
    stacked = jnp.concatenate([up_share, *hi_lo(tail), blank], axis=1).astype(BF)
    share = summed(stacked, Z)
    tail = share[:, half : half + 4] + share[:, half + 4 : half + 8]
    share = jnp.concatenate([share[:, :half], *hi_lo(tail), share[:, half + 8 :]], axis=1)
    gathered = sent_to_all(share.astype(BF), Z).reshape(pool_rows, -1)
    tail = gathered[:, half : half + 8].astype(F32)
    tail = tail[:, :4] + tail[:, 4:]
    tail = jnp.where(z_half == 0, tail[:, :2], tail[:, 2:])
    squares = jnp.concatenate([tail[:, :1], tail[:, 1:]], axis=0)
    pre = dot(pick_one, gathered[:, :half]) + dot(pick_two, pool_pre)
    hidden = jax.nn.silu(pre * lax.rsqrt(squares / D + EPS)).astype(BF)
    last_share = summed(dot(hidden, down_half).astype(BF), CL)

    out_rows = last_share.shape[0]
    own = lax.dynamic_slice_in_dim(tokens, learner * out_rows, out_rows, 0)
    own_two = lax.dynamic_slice_in_dim(tokens, count + learner * out_rows, out_rows, 0)
    choice = lax.broadcasted_iota(jnp.int32, (out_rows, pool_rows), 1)
    own_second = (
        dot((own == choice).astype(BF), carried) + dot((own_two == choice).astype(BF), state_pool)
    ).astype(BF)
    return (own_second.astype(F32) + last_share).astype(BF)[None]


def solution(mesh):
    torus = Mesh(
        mesh.devices.reshape(4, 4, mesh.shape["rollout"], 2, 2), ("y", "x", "zl", "zh", "c")
    )
    return jax.shard_map(
        local,
        mesh=torus,
        in_specs=(
            P(("zl", "zh", "c"), L),
            P(),
            P("zl", L),
            P(L, "zl"),
            P("zl"),
            P(None, "zl"),
            P(None, ("zh", "c"), None),
        ),
        out_specs=P(("zh", "c"), L, "zl"),
        check_vma=False,
    )
```

time: 320 us -> 192 us (0.60)
  the two profiles are of different devices: /device:TPU:2 before, /device:TPU:1 now
where the time goes in v1:
time: 192 us
  waiting for transfers between devices  69.2 us (36%)
  starting transfers between devices  60.8 us (32%)
  blocking collectives  35.2 us (18%)
  matrix products  9.55 us (5%)
  local copies, waits for them, and re-layouts  7.98 us (4%)
  Pallas kernels  6.3 us (3%)
    all_to_all x7, waiting for transfers between devices, swap(): return lax.all_to_all(x, axis, split_axis=0, concat_axis=0, tiled=True)  69.2 us
    all_to_all x7, starting transfers between devices, swap(): return lax.all_to_all(x, axis, split_axis=0, concat_axis=0, tiled=True)  56.1 us
    all_to_all x2, blocking collectives, swap(): return lax.all_to_all(x, axis, split_axis=0, concat_axis=0, tiled=True)  35.2 us
    dot_general x12, matrix products, dot(): return jnp.dot(a, b, preferred_element_type=F32)  8.89 us
    pallas_call x1, Pallas kernels, first_hidden(): pl.pallas_call(functools.partial(first_hidden_kernel, half), out_shape=(s...  6.3 us
    ppermute x1, starting transfers between devices, local(): received = lax.ppermute(sent, 'c', [(0, 1), (1, 0)])  4.66 us
  transfers between devices with their start and end apart: 8, of which 6 were waited for; matrix products, arithmetic and copies ran while one was open for 2% of the time, Pallas kernels for 0%

profile of v1, /device:TPU:1, one launch (start us, length us, event | category | flops | bytes accessed | tf_op | source)
XLA Modules:
  0.0 191.8 jit_solution(13648268343842364168)
XLA Ops:
  0.0 1.5 copy.43
  2.3 0.5 fusion.9
  2.8 0.7 copy.44
  3.5 7.6 %all-to-all-start = ((bf16[16,16,128]{2,1,0:T(8,128)(2,1)}), bf16[16,16,128]{2,1,0:T(8,128)(2,1)S(1)}, u32[]{:S(2)}, u32[]{:S(2)}) async-start(bf16[16,16,128]{2,1,0:T(8,128)(2,1)} %bitcast.4), calls=%async_computation | async-start | bytes 131072 | tf_op jit(solution)/shard_map/all_to_all | solution.py:22
  11.1 4.7 %collective-permute-start = (bf16[256,449]{0,1:T(8,128)(2,1)S(1)}, bf16[256,449]{0,1:T(8,128)(2,1)S(1)}, u32[]{:S(2)}, u32[]{:S(2)}) collective-permute-start(bf16[256,449]{0,1:T(8,128)(2,1)S(1)} %pad_maximum_fusion), channel_id=1, source_target_pairs={{0,1},{1,0},{2,3},{3,2},{4,5},{5,4},{6,7},{7,6},{8,9},{9,8},{10,11... | collective-permute-start | bytes 689672 | tf_op jit(solution)/shard_map/ppermute | solution.py:135
  15.9 1.5 fusion.22
  17.7 0.7 broadcast_in_dim.70
  18.3 7.4 %all-to-all-start.1 = ((bf16[32,16,128]{2,1,0:T(8,128)(2,1)}), bf16[32,16,128]{2,1,0:T(8,128)(2,1)S(1)}, u32[]{:S(2)}, u32[]{:S(2)}) async-start(bf16[32,16,128]{2,1,0:T(8,128)(2,1)} %broadcast_in_dim.70), calls=%async_computation.1 | async-start | bytes 262144 | tf_op jit(solution)/shard_map/all_to_all | solution.py:22
  25.7 7.5 %all-to-all-done.1 = bf16[32,16,128]{2,1,0:T(8,128)(2,1)S(1)} async-done(((bf16[32,16,128]{2,1,0:T(8,128)(2,1)}), bf16[32,16,128]{2,1,0:T(8,128)(2,1)S(1)}, u32[]{:S(2)}, u32[]{:S(2)}) %all-to-all-start.1) | async-done | bytes 131104 | tf_op jit(solution)/shard_map/all_to_all | solution.py:22
  34.3 0.9 concatenate.65
  35.1 13.2 %all-to-all-start.2 = ((bf16[16,8,1152]{2,1,0:T(8,128)(2,1)}), bf16[16,8,1152]{2,1,0:T(8,128)(2,1)S(1)}, u32[]{:S(2)}, u32[]{:S(2)}) async-start(bf16[16,8,1152]{2,1,0:T(8,128)(2,1)} %concatenate.65), calls=%async_computation.2 | async-start | bytes 589824 | tf_op jit(solution)/shard_map/all_to_all | solution.py:22
  48.3 17.6 %all-to-all-done.2 = bf16[16,8,1152]{2,1,0:T(8,128)(2,1)S(1)} async-done(((bf16[16,8,1152]{2,1,0:T(8,128)(2,1)}), bf16[16,8,1152]{2,1,0:T(8,128)(2,1)S(1)}, u32[]{:S(2)}, u32[]{:S(2)}) %all-to-all-start.2) | async-done | bytes 294944 | tf_op jit(solution)/shard_map/all_to_all | solution.py:22
  66.3 0.7 broadcast_in_dim.77
  67.0 7.5 %all-to-all-start.3 = ((bf16[16,8,1152]{2,1,0:T(8,128)(2,1)}), bf16[16,8,1152]{2,1,0:T(8,128)(2,1)S(1)}, u32[]{:S(2)}, u32[]{:S(2)}) async-start(bf16[16,8,1152]{2,1,0:T(8,128)(2,1)} %broadcast_in_dim.77), calls=%async_computation.3 | async-start | bytes 589824 | tf_op jit(solution)/shard_map/all_to_all | solution.py:22
  74.5 16.6 %all-to-all-done.3 = bf16[16,8,1152]{2,1,0:T(8,128)(2,1)S(1)} async-done(((bf16[16,8,1152]{2,1,0:T(8,128)(2,1)}), bf16[16,8,1152]{2,1,0:T(8,128)(2,1)S(1)}, u32[]{:S(2)}, u32[]{:S(2)}) %all-to-all-start.3) | async-done | bytes 294944 | tf_op jit(solution)/shard_map/all_to_all | solution.py:22
  91.1 0.7 copy-done.2
  91.8 6.3 %shard_map.73 = (bf16[128,448]{1,0:T(8,128)(2,1)}, bf16[128,448]{1,0:T(8,128)(2,1)}, bf16[128,448]{1,0:T(8,128)(2,1)}) custom-call(bf16[128,1152]{1,0:T(8,128)(2,1)} %bitcast.58), custom_call_target="tpu_custom_call" | custom-call | tf_op jit(solution)/shard_map/pallas_call | solution.py:109
  98.1 1.2 convolution_convert_fusion.1
  99.4 0.8 reshape.110
  100.1 9.0 %all-to-all-start.4 = ((bf16[32,4,1024]{2,1,0:T(4,128)(2,1)}), bf16[32,4,1024]{2,1,0:T(4,128)(2,1)S(1)}, u32[]{:S(2)}, u32[]{:S(2)}) async-start(bf16[32,4,1024]{2,1,0:T(4,128)(2,1)} %reshape.110), calls=%async_computation.4 | async-start | bytes 524288 | tf_op jit(solution)/shard_map/all_to_all | solution.py:22
  109.3 8.2 %all-to-all-done.4 = bf16[32,4,1024]{2,1,0:T(4,128)(2,1)S(1)} async-done(((bf16[32,4,1024]{2,1,0:T(4,128)(2,1)}), bf16[32,4,1024]{2,1,0:T(4,128)(2,1)S(1)}, u32[]{:S(2)}, u32[]{:S(2)}) %all-to-all-start.4) | async-done | bytes 262176 | tf_op jit(solution)/shard_map/all_to_all | solution.py:22
  117.6 0.8 broadcast_in_dim.78
  118.4 4.7 %all-to-all-start.5 = ((bf16[32,4,1024]{2,1,0:T(4,128)(2,1)}), bf16[32,4,1024]{2,1,0:T(4,128)(2,1)S(1)}, u32[]{:S(2)}, u32[]{:S(2)}) async-start(bf16[32,4,1024]{2,1,0:T(4,128)(2,1)} %broadcast_in_dim.78), calls=%async_computation.5 | async-start | bytes 524288 | tf_op jit(solution)/shard_map/all_to_all | solution.py:22
  123.1 8.3 %all-to-all-done.5 = bf16[32,4,1024]{2,1,0:T(4,128)(2,1)S(1)} async-done(((bf16[32,4,1024]{2,1,0:T(4,128)(2,1)}), bf16[32,4,1024]{2,1,0:T(4,128)(2,1)S(1)}, u32[]{:S(2)}, u32[]{:S(2)}) %all-to-all-start.5) | async-done | bytes 262176 | tf_op jit(solution)/shard_map/all_to_all | solution.py:22
  131.5 1.5 fusion.20
  133.4 0.4 fusion.3
  134.9 17.7 %all_to_all.45 = bf16[16,8,512]{2,1,0:T(8,128)(2,1)S(1)} all-to-all(bf16[16,8,512]{2,1,0:T(8,128)(2,1)S(1)} %maximum_maximum_fusion), channel_id=1, replica_groups=mesh['y'=4,'x'=4,'zl'=8,'zh'=2,'c'=2] {'zl','zh'}, dimensions={0} | all-to-all | bytes 262144 | tf_op jit(solution)/shard_map/all_to_all | solution.py:22
  152.8 17.6 %all_to_all.46 = bf16[16,8,512]{2,1,0:T(8,128)(2,1)S(1)} all-to-all(bf16[16,8,512]{2,1,0:T(8,128)(2,1)S(1)} %broadcast_in_dim.81), channel_id=1, replica_groups=mesh['y'=4,'x'=4,'zl'=8,'zh'=2,'c'=2] {'zl','zh'}, dimensions={0} | all-to-all | bytes 262144 | tf_op jit(solution)/shard_map/all_to_all | solution.py:22
  171.2 1.6 fusion.4
  172.8 6.9 %all-to-all-start.8 = ((bf16[32,8,1024]{2,1,0:T(8,128)(2,1)}), bf16[32,8,1024]{2,1,0:T(8,128)(2,1)S(1)}, u32[]{:S(2)}, u32[]{:S(2)}) async-start(bf16[32,8,1024]{2,1,0:T(8,128)(2,1)} %fusion.4), calls=%async_computation.8 | async-start | bytes 1048576 | tf_op jit(solution)/shard_map/all_to_all | solution.py:22
  180.0 10.9 %all-to-all-done.8 = bf16[32,8,1024]{2,1,0:T(8,128)(2,1)S(1)} async-done(((bf16[32,8,1024]{2,1,0:T(8,128)(2,1)}), bf16[32,8,1024]{2,1,0:T(8,128)(2,1)S(1)}, u32[]{:S(2)}, u32[]{:S(2)}) %all-to-all-start.8) | async-done | bytes 524320 | tf_op jit(solution)/shard_map/all_to_all | solution.py:22
  190.9 0.8 fusion.17
  (74 shorter events, 4.8 us)
Async XLA Ops:
  0.0 98.1 %copy-start = (bf16[896,1024]{1,0:T(8,128)(2,1)S(1)}, bf16[896,1024]{1,0:T(8,128)(2,1)}, u32[]{:S(2)}) copy-start(bf16[896,1024]{1,0:T(8,128)(2,1)} %param.10) | copy-start | bytes 5505028
  0.0 11.1 %copy-start.4 = (s32[2,1,128]{2,1,0:T(1,128)S(1)}, s32[2,1,128]{2,1,0:T(1,128)}, u32[]{:S(2)}) copy-start(s32[2,1,128]{2,1,0:T(1,128)} %param.13) | copy-start | bytes 3076
  1.5 14.3 %copy-start.5 = (bf16[1024]{0:T(1024)(128)(2,1)S(1)}, bf16[1024]{0:T(1024)(128)(2,1)}, u32[]{:S(2)}) copy-start(bf16[1024]{0:T(1024)(128)(2,1)} %param.11) | copy-start | bytes 6148
  1.6 14.4 %copy-start.1 = (bf16[128,1024]{1,0:T(8,128)(2,1)S(1)}, bf16[128,1024]{1,0:T(8,128)(2,1)}, u32[]{:S(2)}) copy-start(bf16[128,1024]{1,0:T(8,128)(2,1)} %param.12) | copy-start | bytes 786436
  3.5 14.2 %all-to-all-start = ((bf16[16,16,128]{2,1,0:T(8,128)(2,1)}), bf16[16,16,128]{2,1,0:T(8,128)(2,1)S(1)}, u32[]{:S(2)}, u32[]{:S(2)}) async-start(bf16[16,16,128]{2,1,0:T(8,128)(2,1)} %bitcast.4), calls=%async_computation | async-start | bytes 131072 | tf_op jit(solution)/shard_map/all_to_all | solution.py:22
  11.1 22.7 %collective-permute-start = (bf16[256,449]{0,1:T(8,128)(2,1)S(1)}, bf16[256,449]{0,1:T(8,128)(2,1)S(1)}, u32[]{:S(2)}, u32[]{:S(2)}) collective-permute-start(bf16[256,449]{0,1:T(8,128)(2,1)S(1)} %pad_maximum_fusion), channel_id=1, source_target_pairs={{0,1},{1,0},{2,3},{3,2},{4,5},{5,4},{6,7},{7,6},{8,9},{9,8},{10,11... | collective-permute-start | bytes 689672 | tf_op jit(solution)/shard_map/ppermute | solution.py:135
  18.3 14.9 %all-to-all-start.1 = ((bf16[32,16,128]{2,1,0:T(8,128)(2,1)}), bf16[32,16,128]{2,1,0:T(8,128)(2,1)S(1)}, u32[]{:S(2)}, u32[]{:S(2)}) async-start(bf16[32,16,128]{2,1,0:T(8,128)(2,1)} %broadcast_in_dim.70), calls=%async_computation.1 | async-start | bytes 262144 | tf_op jit(solution)/shard_map/all_to_all | solution.py:22
  35.1 30.8 %all-to-all-start.2 = ((bf16[16,8,1152]{2,1,0:T(8,128)(2,1)}), bf16[16,8,1152]{2,1,0:T(8,128)(2,1)S(1)}, u32[]{:S(2)}, u32[]{:S(2)}) async-start(bf16[16,8,1152]{2,1,0:T(8,128)(2,1)} %concatenate.65), calls=%async_computation.2 | async-start | bytes 589824 | tf_op jit(solution)/shard_map/all_to_all | solution.py:22
  67.0 24.1 %all-to-all-start.3 = ((bf16[16,8,1152]{2,1,0:T(8,128)(2,1)}), bf16[16,8,1152]{2,1,0:T(8,128)(2,1)S(1)}, u32[]{:S(2)}, u32[]{:S(2)}) async-start(bf16[16,8,1152]{2,1,0:T(8,128)(2,1)} %broadcast_in_dim.77), calls=%async_computation.3 | async-start | bytes 589824 | tf_op jit(solution)/shard_map/all_to_all | solution.py:22
  91.1 0.7 copy-start.2
  100.1 17.3 %all-to-all-start.4 = ((bf16[32,4,1024]{2,1,0:T(4,128)(2,1)}), bf16[32,4,1024]{2,1,0:T(4,128)(2,1)S(1)}, u32[]{:S(2)}, u32[]{:S(2)}) async-start(bf16[32,4,1024]{2,1,0:T(4,128)(2,1)} %reshape.110), calls=%async_computation.4 | async-start | bytes 524288 | tf_op jit(solution)/shard_map/all_to_all | solution.py:22
  118.4 13.0 %all-to-all-start.5 = ((bf16[32,4,1024]{2,1,0:T(4,128)(2,1)}), bf16[32,4,1024]{2,1,0:T(4,128)(2,1)S(1)}, u32[]{:S(2)}, u32[]{:S(2)}) async-start(bf16[32,4,1024]{2,1,0:T(4,128)(2,1)} %broadcast_in_dim.78), calls=%async_computation.5 | async-start | bytes 524288 | tf_op jit(solution)/shard_map/all_to_all | solution.py:22
  131.5 3.0 %copy-start.3 = (bf16[128,448]{1,0:T(8,128)(2,1)S(1)}, bf16[128,448]{1,0:T(8,128)(2,1)}, u32[]{:S(2)}) copy-start(bf16[128,448]{1,0:T(8,128)(2,1)} %get-tuple-element.9) | copy-start | bytes 344068
  133.8 37.4 %copy-start.6 = (bf16[128,448]{1,0:T(8,128)(2,1)S(1)}, bf16[128,448]{1,0:T(8,128)(2,1)}, u32[]{:S(2)}) copy-start(bf16[128,448]{1,0:T(8,128)(2,1)} %get-tuple-element.10) | copy-start | bytes 344068
  172.8 18.0 %all-to-all-start.8 = ((bf16[32,8,1024]{2,1,0:T(8,128)(2,1)}), bf16[32,8,1024]{2,1,0:T(8,128)(2,1)S(1)}, u32[]{:S(2)}, u32[]{:S(2)}) async-start(bf16[32,8,1024]{2,1,0:T(8,128)(2,1)} %fusion.4), calls=%async_computation.8 | async-start | bytes 1048576 | tf_op jit(solution)/shard_map/all_to_all | solution.py:22

commit v2 on v1

v2 whole, which is shorter than its diff:
```python
import functools

import jax
import jax.numpy as jnp
from jax import lax
from jax.experimental import pallas as pl
from jax.experimental.pallas import tpu as pltpu
from jax.sharding import Mesh
from jax.sharding import PartitionSpec as P

D = 8192
RANK = 128
EPS = 1e-05
L = ("y", "x")
CL = ("c", "y", "x")
Z = ("zl", "zh")
BF = jnp.bfloat16
F32 = jnp.float32


def swap(x, axis):
    return lax.all_to_all(x, axis, split_axis=0, concat_axis=0, tiled=True)


def sent_to_all(x, axis):
    return swap(jnp.broadcast_to(x, (lax.axis_size(axis), *x.shape)), axis)


def dot(a, b):
    return jnp.dot(a, b, preferred_element_type=F32)


def dot_t(a, b):
    return lax.dot_general(a, b, (((0,), (0,)), ((), ())), preferred_element_type=F32)


def hi_lo(x):
    hi = x.astype(BF).astype(F32)
    return hi, x - hi


def diagonal_offset(rows, first):
    row = first + lax.broadcasted_iota(jnp.int32, (rows, RANK), 0)
    col = lax.broadcasted_iota(jnp.int32, (rows, RANK), 1)
    return (col - row) & (RANK - 1)


def packed(gram, squares, offset):
    hi, lo = hi_lo(squares)
    rest = jnp.where(offset == RANK - 1, lo, jnp.where(offset == RANK - 2, hi, 0.0))
    return jnp.where(offset <= RANK // 2, gram, rest)


def unpacked_squares(gram, offset):
    return jnp.sum(jnp.where(offset >= RANK - 2, gram, 0.0), axis=1, keepdims=True)


def precise(a, b):
    return jnp.dot(a, b, precision=lax.Precision.HIGHEST, preferred_element_type=F32)


def silu(x):
    return x / (1.0 + jnp.exp(-x))


def total(ref):
    return jnp.sum(ref[...].astype(F32), axis=0)


def call(kernel, shapes, place, *arrays, limit=24):
    specs = [pl.BlockSpec(memory_space=pltpu.SMEM)]
    specs += [pl.BlockSpec(memory_space=pltpu.VMEM)] * len(arrays)
    return pl.pallas_call(
        kernel,
        out_shape=tuple(jax.ShapeDtypeStruct(shape, BF) for shape in shapes),
        in_specs=specs,
        out_specs=(pl.BlockSpec(memory_space=pltpu.VMEM),) * len(shapes),
        compiler_params=pltpu.CompilerParams(vmem_limit_bytes=limit * 1024 * 1024),
    )(place, *arrays)


def range_kernel(place, delta_ref, tokens_ref, part_ref, kept_ref, sent_ref):
    core = place[0]
    rows, cols = delta_ref.shape
    half = cols // 2
    row_index = place[3] + lax.broadcasted_iota(jnp.int32, (cols, RANK), 0)
    col_index = lax.broadcasted_iota(jnp.int32, (cols, RANK), 1)
    hashed = row_index * RANK + col_index + place[4]
    hashed = hashed * 1103515245 + 12345
    hashed = hashed ^ lax.shift_right_logical(hashed, jnp.int32(16))
    hashed = hashed * 73244475
    hashed = hashed ^ lax.shift_right_logical(hashed, jnp.int32(15))
    parity = lax.shift_right_logical(hashed, jnp.int32(11)) & 1
    signs = (2 * parity - 1).astype(F32).astype(BF)
    delta = delta_ref[...].astype(BF)
    part_ref[...] = dot(delta, signs).astype(BF).reshape(part_ref.shape)
    left, right = delta[:, :half], delta[:, half:]
    kept_ref[...] = jnp.where(core == 0, left, right)
    sent_ref[:, :half] = jnp.where(core == 0, right, left)
    spare = sent_ref.shape[1] - half
    sent_ref[:, half:] = jnp.broadcast_to(tokens_ref[...].astype(F32), (rows, spare)).astype(BF)


def moved_kernel(place, basis_ref, kept_ref, got_ref, pool_ref, up_ref, squares_ref, out_ref):
    core = place[0]
    rows, half = kept_ref.shape
    count = basis_ref.shape[0] // 2
    own = basis_ref[pl.ds(core * count, count)].reshape(rows, RANK)
    other = basis_ref[pl.ds((1 - core) * count, count)].reshape(rows, RANK)
    basis = basis_ref[...].reshape(2 * rows, RANK)

    def put(first, values):
        values = values.astype(BF)
        out_ref[:, :, first : first + values.shape[1]] = values.reshape(
            *out_ref.shape[:2], values.shape[1]
        )

    moved = dot_t(own, kept_ref[...]) + dot_t(other, got_ref[:, :half])
    both = jnp.concatenate([moved.astype(BF), up_ref[...]], axis=1)
    put(0, both)
    put(2 * half, packed(dot_t(basis, basis), squares_ref[...], diagonal_offset(RANK, 0)))
    put(2 * half + RANK, dot(pool_ref[...], basis))


def share_kernel(place, parts_ref, out_ref):
    share = total(parts_ref)
    rows, width = share.shape
    first = width - 2 * RANK
    offset = diagonal_offset(rows, place[2] * rows)
    gram = share[:, first : first + RANK]
    gram = packed(gram, unpacked_squares(gram, offset), offset)
    share = jnp.concatenate([share[:, :first], gram, share[:, first + RANK :]], axis=1)
    out_ref[...] = jnp.broadcast_to(share.astype(BF), out_ref.shape)


def first_kernel(place, z_ref, down_ref, step_ref, coef_ref, pre_ref):
    half = coef_ref.shape[1]
    gathered = z_ref[...].reshape(RANK, z_ref.shape[2])
    gram = gathered[:, 2 * half : 2 * half + RANK].astype(F32)
    row = lax.broadcasted_iota(jnp.int32, (RANK, RANK), 0)
    col = lax.broadcasted_iota(jnp.int32, (RANK, RANK), 1)
    offset = (col - row) & (RANK - 1)
    squares = unpacked_squares(gram, offset)
    gram = jnp.where(offset <= RANK // 2, gram, gram.T)
    eye = jnp.where(row == col, 1.0, 0.0)
    on_diag = gram * eye
    scale_col = lax.rsqrt(jnp.sum(on_diag, axis=1, keepdims=True))
    scale_row = lax.rsqrt(jnp.sum(on_diag, axis=0, keepdims=True))
    unit = gram * scale_col * scale_row
    bound = jnp.max(jnp.sum(jnp.abs(unit), axis=1, keepdims=True), axis=0, keepdims=True)
    step = 2.0 / (1.0 + bound)
    start = step * (2.0 * eye - step * unit)

    def going(state):
        count, error, _ = state
        return jnp.logical_and(count < 40, error > 2e-4)

    def refine(state):
        count, _, inverse = state
        left = eye - precise(unit, inverse)
        return count + 1, jnp.sum(left * left), inverse + precise(inverse, left)

    _, _, inverse = lax.while_loop(going, refine, (0, jnp.float32(1.0), start))
    moved = gathered[:, :half].astype(F32) * scale_col
    coef = (precise(inverse, moved) * scale_col).astype(BF)
    coef_ref[...] = coef
    pre = gathered[:, half : 2 * half].astype(F32) + dot(gathered[:, 2 * half + RANK :], coef)
    pre_ref[...] = pre.astype(BF)
    hidden = silu(pre * lax.rsqrt(squares / D + EPS)).astype(BF)
    result = dot(hidden, down_ref[...]).astype(BF)
    count, rows, width = step_ref.shape
    step_ref[: count // 2] = result[:, :width].reshape(count // 2, rows, width)
    step_ref[count // 2 :] = result[:, width:].reshape(count // 2, rows, width)


def second_kernel(
    place, step_ref, pool_ref, gain_ref, up_ref, basis_ref, coef_ref, pick_ref, own_ref, out_ref, rows_ref
):
    z_half = place[1]
    count, rows, width = step_ref.shape
    pool_rows = pool_ref.shape[0]
    half = coef_ref.shape[1]
    basis = basis_ref[...].reshape(width, RANK)
    step = step_ref[...].astype(F32).reshape(2, pool_rows, width)
    pool = pool_ref[...]
    left = (pool[:, :width].astype(F32) + step[0]).astype(BF)
    right = (pool[:, width:].astype(F32) + step[1]).astype(BF)
    carried = jnp.concatenate([left, right], axis=1)
    gained = jnp.where(z_half == 0, left, right).astype(F32) * gain_ref[...]
    gained = gained.astype(BF)
    up = dot(gained, up_ref[...]) + dot(dot(gained, basis).astype(BF), coef_ref[...])

    def second(pick):
        return (dot(pick[0], carried) + dot(pick[1], pool)).astype(BF)

    wide = second(pick_ref).astype(F32)
    squares = jnp.sum(wide * wide, axis=1, keepdims=True)
    lane = lax.broadcasted_iota(jnp.int32, (pool_rows, out_ref.shape[2] - half), 1)
    first = 4 * z_half
    tail = jnp.zeros(lane.shape, F32)
    for place_in, value in enumerate((*hi_lo(squares[:pool_rows]), *hi_lo(squares[pool_rows:]))):
        tail = jnp.where(lane == first + place_in, value, tail)
    both = jnp.concatenate([up.astype(BF), tail.astype(BF)], axis=1)
    out_ref[...] = both.reshape(out_ref.shape)
    rows_ref[...] = second(own_ref)


def second_share_kernel(half, place, parts_ref, out_ref):
    share = total(parts_ref)
    lane = lax.broadcasted_iota(jnp.int32, share.shape, 1)
    out = share
    for first in range(half, half + 8, 2):
        whole = jnp.where(jnp.logical_or(lane == first, lane == first + 1), share, 0.0)
        hi, lo = hi_lo(jnp.sum(whole, axis=1, keepdims=True))
        out = jnp.where(lane == first, hi, jnp.where(lane == first + 1, lo, out))
    out_ref[...] = jnp.broadcast_to(out.astype(BF), out_ref.shape)


def last_kernel(place, z_ref, pre_ref, pick_ref, down_ref, out_ref):
    z_half = place[1]
    half = pre_ref.shape[1]
    pool_rows = pre_ref.shape[0]
    gathered = z_ref[...].reshape(pool_rows, z_ref.shape[2])
    lane = lax.broadcasted_iota(jnp.int32, gathered.shape, 1)

    def squares(first):
        first = half + 4 * z_half + first
        chosen = jnp.logical_or(lane == first, lane == first + 1)
        return jnp.sum(jnp.where(chosen, gathered.astype(F32), 0.0), axis=1, keepdims=True)

    scale = lax.rsqrt(jnp.concatenate([squares(0), squares(2)], axis=0) / D + EPS)
    pre = dot(pick_ref[0], gathered[:, :half]) + dot(pick_ref[1], pre_ref[...])
    hidden = silu(pre * scale).astype(BF)
    out_ref[...] = dot(hidden, down_ref[...]).astype(BF).reshape(out_ref.shape)


def local(weight_delta, sketch_seed, up_weight, down_weight, norm_gain, state_pool, token_rows):
    core = lax.axis_index("c")
    z_half = lax.axis_index("zh")
    learner = lax.axis_index(L)
    rows, cols = weight_delta.shape
    half = cols // 2
    width = 2 * rows
    count = state_pool.shape[0]
    out_rows = count // 16
    place = jnp.stack(
        [core, z_half, lax.axis_index(Z), learner * cols, sketch_seed[0] * 7919]
    ).astype(jnp.int32)

    tokens = token_rows[:, 0, :]
    part, kept, sent = call(
        range_kernel,
        ((16, rows // 16, RANK), (rows, half), (rows, half + 64)),
        place,
        weight_delta,
        tokens.reshape(-1, 1),
    )
    received = lax.ppermute(sent, "c", [(0, 1), (1, 0)])
    parts = swap(part, L)

    def own_half(x):
        return jnp.where(core == 0, x[:, :half], x[:, half:])

    pool_half = lax.dynamic_slice_in_dim(state_pool, z_half * width, width, 1).astype(F32)
    gain_half = lax.dynamic_slice_in_dim(norm_gain, z_half * width, width, 0).astype(F32)[None]
    up_own = own_half(lax.dynamic_slice_in_dim(up_weight, z_half * width, width, 0))
    down_own = lax.dynamic_slice_in_dim(down_weight, core * half, half, 0)
    pool_gained = (pool_half * gain_half).astype(BF)
    pool_up = dot(pool_gained, up_own).astype(BF)
    squares = jnp.sum(pool_half * pool_half, axis=1, keepdims=True)
    mine = tokens[:, :, None]
    theirs = received[:, half : half + 1].astype(jnp.int32).reshape(2, count, 1)
    both = jnp.where(
        core == 0, jnp.concatenate([mine, theirs], 1), jnp.concatenate([theirs, mine], 1)
    )
    picks = (both == lax.broadcasted_iota(jnp.int32, (2, 2 * count, count), 2)).astype(BF)
    own = lax.dynamic_slice_in_dim(mine, learner * out_rows, out_rows, 1)
    own_picks = (own == lax.broadcasted_iota(jnp.int32, (2, out_rows, count), 2)).astype(BF)

    range_share = jnp.sum(parts.astype(F32), axis=0).astype(BF)
    side = (kept, received, pool_gained, pool_up, squares, gain_half, up_own, down_own, picks, own_picks, place, state_pool)
    range_share, side = lax.optimization_barrier((range_share, side))
    kept, received, pool_gained, pool_up, squares, gain_half, up_own, down_own, picks, own_picks, place, pool = side

    basis = sent_to_all(range_share, CL)
    (stacked,) = call(
        moved_kernel,
        ((16, count // 16, 2 * half + 2 * RANK),),
        place, basis, kept, received, pool_gained, pool_up, squares,
    )
    (share,) = call(share_kernel, (stacked.shape,), place, swap(stacked, Z))
    step_part, coef, pool_pre = call(
        first_kernel,
        ((32, count // 16, width), (RANK, half), (count, half)),
        place, swap(share, Z), down_own,
    )
    step_share = jnp.sum(swap(step_part, CL).astype(F32), axis=0).astype(BF)
    step = sent_to_all(step_share, CL)
    stacked, own_second = call(
        second_kernel,
        ((16, count // 16, half + 64), (out_rows, 2 * width)),
        place, step, pool, gain_half, up_own, basis, coef, picks, own_picks,
    )
    (share,) = call(
        functools.partial(second_share_kernel, half), (stacked.shape,), place, swap(stacked, Z)
    )
    (last,) = call(
        last_kernel,
        ((32, out_rows, 2 * width),),
        place, swap(share, Z), pool_pre, picks, down_own,
    )
    last_share = jnp.sum(swap(last, CL).astype(F32), axis=0)
    return (own_second.astype(F32) + last_share).astype(BF)[None]


def solution(mesh):
    torus = Mesh(
        mesh.devices.reshape(4, 4, mesh.shape["rollout"], 2, 2), ("y", "x", "zl", "zh", "c")
    )
    return jax.shard_map(
        local,
        mesh=torus,
        in_specs=(
            P(("zl", "zh", "c"), L),
            P(),
            P("zl", L),
            P(L, "zl"),
            P("zl"),
            P(None, "zl"),
            P(None, ("zh", "c"), None),
        ),
        out_specs=P(("zh", "c"), L, "zl"),
        check_vma=False,
    )
```

time: 192 us -> 197 us (1.026)
  blocking collectives: 35.2 us -> 137 us
  waiting for transfers between devices: 69.2 us -> 6.8 us
  starting transfers between devices: 60.8 us -> 19.6 us
  matrix products: 9.55 us -> 0.9 us
  other arithmetic: 1.54 us -> 7.51 us
  Pallas kernels: 6.3 us -> 11.9 us
  local copies, waits for them, and re-layouts: 7.98 us -> 11.6 us
    all_to_all x2 -> x7, blocking collectives: 35.2 us -> 137 us  [swap(): return lax.all_to_all(x, axis, split_axis=0, concat_axis=0, tiled=True)]
    all_to_all x7 -> x2, waiting for transfers between devices: 69.2 us -> 6.8 us  [swap(): return lax.all_to_all(x, axis, split_axis=0, concat_axis=0, tiled=True)]
    all_to_all x7 -> x2, starting transfers between devices: 56.1 us -> 14.9 us  [swap(): return lax.all_to_all(x, axis, split_axis=0, concat_axis=0, tiled=True)]
    dot_general x12 -> x1, matrix products: 8.89 us -> 0.9 us  [dot(): return jnp.dot(a, b, preferred_element_type=F32)]
    pallas_call x1 -> x7, Pallas kernels: 6.3 us -> 11.9 us  [call(): pl.pallas_call(kernel, out_shape=tuple((jax.ShapeDtypeStruct(shape, BF) f...]
    unnamed x15 -> x26, local copies, waits for them, and re-layouts: 2.26 us -> 7.73 us
    reduce_sum x7 -> x4, other arithmetic: 0.6 us -> 2.73 us  [the longest x1 1.6 us: local(): step_share = jnp.sum(swap(step_part, CL).astype(F32), axis=0).astype(BF)]
  transfers between devices with their start and end apart: 8 -> 3, of which waited for: 6 -> 1; matrix products, arithmetic and copies ran while one was open for 2% -> 3% of each run, Pallas kernels for 0% -> 0%
where the time goes in v2:
time: 197 us; the launch traced here: 196 us
  blocking collectives  137 us (70%)
  starting transfers between devices  19.6 us (10%)
  Pallas kernels  11.9 us (6%)
  local copies, waits for them, and re-layouts  11.6 us (6%)
  other arithmetic  7.51 us (4%)
  waiting for transfers between devices  6.8 us (3%)
    all_to_all x7, blocking collectives, swap(): return lax.all_to_all(x, axis, split_axis=0, concat_axis=0, tiled=True)  137 us
    all_to_all x2, starting transfers between devices, swap(): return lax.all_to_all(x, axis, split_axis=0, concat_axis=0, tiled=True)  14.9 us
    pallas_call x7, Pallas kernels, call(): pl.pallas_call(kernel, out_shape=tuple((jax.ShapeDtypeStruct(shape, BF) f...  11.9 us
    unnamed x26, local copies, waits for them, and re-layouts  7.73 us
    all_to_all x2, waiting for transfers between devices, swap(): return lax.all_to_all(x, axis, split_axis=0, concat_axis=0, tiled=True)  6.8 us
    ppermute x1, starting transfers between devices, local(): received = lax.ppermute(sent, 'c', [(0, 1), (1, 0)])  4.66 us
  transfers between devices with their start and end apart: 3, of which 1 were waited for; matrix products, arithmetic and copies ran while one was open for 3% of the time, Pallas kernels for 0%

profile of v2, /device:TPU:1, one launch (start us, length us, event | category | flops | bytes accessed | tf_op | source)
XLA Modules:
  0.0 196.4 jit_solution(12126968727822024258)
XLA Ops:
  0.8 0.8 copy.10.tokens_ref
  1.7 1.2 copy-done.2
  2.9 1.7 shard_map.73
  5.3 7.6 %all-to-all-start = ((bf16[16,16,128]{2,1,0:T(8,128)(2,1)}), bf16[16,16,128]{2,1,0:T(8,128)(2,1)S(1)}, u32[]{:S(2)}, u32[]{:S(2)}) async-start(bf16[16,16,128]{2,1,0:T(8,128)(2,1)} %get-tuple-element.26), calls=%async_computation | async-start | bytes 131072 | tf_op jit(solution)/shard_map/all_to_all | solution.py:22
  12.9 4.7 %collective-permute-start = (bf16[256,512]{1,0:T(8,128)(2,1)}, bf16[256,512]{1,0:T(8,128)(2,1)}, u32[]{:S(2)}, u32[]{:S(2)}) collective-permute-start(bf16[256,512]{1,0:T(8,128)(2,1)} %get-tuple-element.28), channel_id=1, source_target_pairs={{0,1},{1,0},{2,3},{3,2},{4,5},{5,4},{6,7},{7,6},{8,9},{9,8},{10,11... | collective-permute-start | bytes 786440 | tf_op jit(solution)/shard_map/ppermute | solution.py:258
  17.6 0.8 constant_dynamic-slice_fusion
  18.4 0.8 dynamic-slice_convert_fusion
  19.1 1.0 fusion.1
  20.1 1.5 dynamic-slice_select_fusion.up_ref
  21.7 0.9 convolution_convert_fusion.up_ref
  22.8 1.0 convert_reduce_fusion.1
  23.8 0.8 fusion.2.pick_ref
  25.3 7.3 %all-to-all-start.1 = ((bf16[32,16,128]{2,1,0:T(8,128)(2,1)}), bf16[32,16,128]{2,1,0:T(8,128)(2,1)S(1)}, u32[]{:S(2)}, u32[]{:S(2)}) async-start(bf16[32,16,128]{2,1,0:T(8,128)(2,1)} %broadcast_in_dim.17), calls=%async_computation.1 | async-start | bytes 262144 | tf_op jit(solution)/shard_map/all_to_all | solution.py:22
  33.3 6.8 %all-to-all-done.1.basis_ref = bf16[32,16,128]{2,1,0:T(8,128)(2,1)S(1)} async-done(((bf16[32,16,128]{2,1,0:T(8,128)(2,1)}), bf16[32,16,128]{2,1,0:T(8,128)(2,1)S(1)}, u32[]{:S(2)}, u32[]{:S(2)}) %all-to-all-start.1) | async-done | bytes 131104 | tf_op jit(solution)/shard_map/all_to_all | solution.py:22
  40.1 0.9 copy-done.4
  41.0 0.8 copy-done.5
  41.9 0.9 copy-done.7
  42.8 1.3 shard_map.74
  44.1 30.7 %all_to_all.45.parts_ref = bf16[16,8,1152]{2,1,0:T(8,128)(2,1)S(1)} all-to-all(bf16[16,8,1152]{2,1,0:T(8,128)(2,1)S(1)} %shard_map.74), channel_id=1, replica_groups=mesh['y'=4,'x'=4,'zl'=8,'zh'=2,'c'=2] {'zl','zh'}, dimensions={0} | all-to-all | bytes 589824 | tf_op jit(solution)/shard_map/all_to_all | solution.py:22
  75.5 23.9 %all_to_all.46.z_ref = bf16[16,8,1152]{2,1,0:T(8,128)(2,1)S(1)} all-to-all(bf16[16,8,1152]{2,1,0:T(8,128)(2,1)S(1)} %shard_map.75), channel_id=1, replica_groups=mesh['y'=4,'x'=4,'zl'=8,'zh'=2,'c'=2] {'zl','zh'}, dimensions={0} | all-to-all | bytes 589824 | tf_op jit(solution)/shard_map/all_to_all | solution.py:22
  99.4 4.8 %shard_map.76 = (bf16[32,8,512]{2,1,0:T(8,128)(2,1)S(1)}, bf16[128,448]{1,0:T(8,128)(2,1)S(1)}, bf16[128,448]{1,0:T(8,128)(2,1)S(1)}) custom-call(s32[5]{0:T(128)S(1)} %stack.20.place, bf16[16,8,1152]{2,1,0:T(8,128)(2,1)S(1)} %all_to_all.46.z_ref, bf16[448,1024]{1,0:T(8,128)(2,1)S(1)} %constant_dynamic-slice_fusion.1.down_ref), custom_call_target="tpu_custom_call" | custom-call | tf_op jit(solution)/shard_map/pallas_call | solution.py:73
  105.6 17.1 %all_to_all.47 = bf16[32,8,512]{2,1,0:T(8,128)(2,1)} all-to-all(bf16[32,8,512]{2,1,0:T(8,128)(2,1)S(1)} %get-tuple-element.37), channel_id=1, replica_groups=mesh['y'=4,'x'=4,'zl'=8,'zh'=2,'c'=2] {'c','y','x'}, dimensions={0} | all-to-all | bytes 524288 | tf_op jit(solution)/shard_map/all_to_all | solution.py:22
  122.7 1.6 reduce_sum.44
  124.3 0.7 broadcast_in_dim.18
  125.0 12.4 %all_to_all.48.step_ref = bf16[32,8,512]{2,1,0:T(8,128)(2,1)S(1)} all-to-all(bf16[32,8,512]{2,1,0:T(8,128)(2,1)S(1)} %broadcast_in_dim.18), channel_id=1, replica_groups=mesh['y'=4,'x'=4,'zl'=8,'zh'=2,'c'=2] {'c','y','x'}, dimensions={0} | all-to-all | bytes 524288 | tf_op jit(solution)/shard_map/all_to_all | solution.py:22
  137.5 0.9 copy-done.3
  138.4 0.9 copy-done.11
  139.3 1.4 shard_map.77
  140.7 17.7 %all_to_all.49.parts_ref = bf16[16,8,512]{2,1,0:T(8,128)(2,1)S(1)} all-to-all(bf16[16,8,512]{2,1,0:T(8,128)(2,1)S(1)} %get-tuple-element.45), channel_id=1, replica_groups=mesh['y'=4,'x'=4,'zl'=8,'zh'=2,'c'=2] {'zl','zh'}, dimensions={0} | all-to-all | bytes 262144 | tf_op jit(solution)/shard_map/all_to_all | solution.py:22
  159.1 17.6 %all_to_all.50.z_ref = bf16[16,8,512]{2,1,0:T(8,128)(2,1)S(1)} all-to-all(bf16[16,8,512]{2,1,0:T(8,128)(2,1)S(1)} %shard_map.78), channel_id=1, replica_groups=mesh['y'=4,'x'=4,'zl'=8,'zh'=2,'c'=2] {'zl','zh'}, dimensions={0} | all-to-all | bytes 262144 | tf_op jit(solution)/shard_map/all_to_all | solution.py:22
  176.7 1.3 shard_map.79
  177.9 17.8 %all_to_all.51 = bf16[32,8,1024]{2,1,0:T(8,128)(2,1)S(1)} all-to-all(bf16[32,8,1024]{2,1,0:T(8,128)(2,1)S(1)} %shard_map.79), channel_id=1, replica_groups=mesh['y'=4,'x'=4,'zl'=8,'zh'=2,'c'=2] {'c','y','x'}, dimensions={0} | all-to-all | bytes 1048576 | tf_op jit(solution)/shard_map/all_to_all | solution.py:22
  (33 shorter events, 5.7 us)
Async XLA Ops:
  0.0 22.7 %copy-start = (bf16[896,1024]{1,0:T(8,128)(2,1)S(1)}, bf16[896,1024]{1,0:T(8,128)(2,1)}, u32[]{:S(2)}) copy-start(bf16[896,1024]{1,0:T(8,128)(2,1)} %param.10) | copy-start | bytes 5505028
  1.7 1.2 copy-start.2
  4.6 0.7 copy-start.6
  5.3 17.4 %all-to-all-start = ((bf16[16,16,128]{2,1,0:T(8,128)(2,1)}), bf16[16,16,128]{2,1,0:T(8,128)(2,1)S(1)}, u32[]{:S(2)}, u32[]{:S(2)}) async-start(bf16[16,16,128]{2,1,0:T(8,128)(2,1)} %get-tuple-element.26), calls=%async_computation | async-start | bytes 131072 | tf_op jit(solution)/shard_map/all_to_all | solution.py:22
  12.9 9.8 %collective-permute-start = (bf16[256,512]{1,0:T(8,128)(2,1)}, bf16[256,512]{1,0:T(8,128)(2,1)}, u32[]{:S(2)}, u32[]{:S(2)}) collective-permute-start(bf16[256,512]{1,0:T(8,128)(2,1)} %get-tuple-element.28), channel_id=1, source_target_pairs={{0,1},{1,0},{2,3},{3,2},{4,5},{5,4},{6,7},{7,6},{8,9},{9,8},{10,11... | collective-permute-start | bytes 786440 | tf_op jit(solution)/shard_map/ppermute | solution.py:258
  20.1 3.7 %copy-start.12 = (s32[2,1,128]{2,1,0:T(1,128)S(1)}, s32[2,1,128]{2,1,0:T(1,128)}, u32[]{:S(2)}) copy-start(s32[2,1,128]{2,1,0:T(1,128)} %param.13) | copy-start | bytes 3076
  25.3 14.8 %all-to-all-start.1 = ((bf16[32,16,128]{2,1,0:T(8,128)(2,1)}), bf16[32,16,128]{2,1,0:T(8,128)(2,1)S(1)}, u32[]{:S(2)}, u32[]{:S(2)}) async-start(bf16[32,16,128]{2,1,0:T(8,128)(2,1)} %broadcast_in_dim.17), calls=%async_computation.1 | async-start | bytes 262144 | tf_op jit(solution)/shard_map/all_to_all | solution.py:22
  40.1 0.9 copy-start.4
  41.0 0.8 copy-start.5
  41.9 0.9 copy-start.7
  75.5 61.9 %copy-start.1 = (bf16[2,256,128]{2,1,0:T(8,128)(2,1)S(1)}, bf16[2,256,128]{2,1,0:T(8,128)(2,1)}, u32[]{:S(2)}) copy-start(bf16[2,256,128]{2,1,0:T(8,128)(2,1)} %fusion.2.pick_ref) | copy-start | bytes 393220
  104.3 0.7 copy-start.8
  104.9 0.7 copy-start.10
  124.3 52.4 %copy-start.9 = (bf16[128,448]{1,0:T(8,128)(2,1)S(1)}, bf16[128,448]{1,0:T(8,128)(2,1)}, u32[]{:S(2)}) copy-start(bf16[128,448]{1,0:T(8,128)(2,1)} %copy-done.8) | copy-start | bytes 344068
  137.5 1.0 copy-start.3
  138.4 0.9 copy-start.11

commit v3 on v2

--- a/solution.py
+++ b/solution.py
@@ -67,22 +67,66 @@
     return jnp.sum(ref[...].astype(F32), axis=0)
 
 
-def call(kernel, shapes, place, *arrays, limit=24):
+HBM = pl.BlockSpec(memory_space=pltpu.HBM)
+VMEM = pl.BlockSpec(memory_space=pltpu.VMEM)
+
+
+def call(kernel, shapes, place, *arrays, hbm=None, scratch=()):
     specs = [pl.BlockSpec(memory_space=pltpu.SMEM)]
-    specs += [pl.BlockSpec(memory_space=pltpu.VMEM)] * len(arrays)
+    if hbm is not None:
+        arrays = (hbm, *arrays)
+        specs += [HBM]
+        scratch = (*scratch, pltpu.SemaphoreType.DMA((2,)))
+    specs += [VMEM] * (len(arrays) - (hbm is not None))
     return pl.pallas_call(
         kernel,
         out_shape=tuple(jax.ShapeDtypeStruct(shape, BF) for shape in shapes),
         in_specs=specs,
-        out_specs=(pl.BlockSpec(memory_space=pltpu.VMEM),) * len(shapes),
-        compiler_params=pltpu.CompilerParams(vmem_limit_bytes=limit * 1024 * 1024),
+        out_specs=(VMEM,) * len(shapes),
+        scratch_shapes=scratch,
+        compiler_params=pltpu.CompilerParams(vmem_limit_bytes=16 * 1024 * 1024),
     )(place, *arrays)
 
 
-def range_kernel(place, delta_ref, tokens_ref, part_ref, kept_ref, sent_ref):
+def column(row):
+    return jnp.broadcast_to(row, (RANK, RANK)).T
+
+
+def chosen(tokens, step):
+    count = tokens.shape[0] // 2
+    rows = tokens[step * count : (step + 1) * count].astype(F32)
+    lane = lax.broadcasted_iota(jnp.int32, (count, RANK), 1).astype(F32)
+    return jnp.where(rows == lane, 1.0, 0.0).astype(BF)
+
+
+def picks(place, kept_ref, got_ref, step):
+    half = kept_ref.shape[1] - RANK // 2
+    mine = chosen(kept_ref[:, half : half + 1], step)
+    theirs = chosen(got_ref[:, half : half + 1], step)
+    first = place[0] == 0
+    return jnp.concatenate(
+        [jnp.where(first, mine, theirs), jnp.where(first, theirs, mine)], axis=0
+    )
+
+
+def own_half(place, x):
+    half = x.shape[1] // 2
+    return jnp.where(place[0] == 0, x[:, :half], x[:, half:])
+
+
+def range_kernel(place, delta_hbm, tokens_ref, part_ref, kept_ref, sent_ref, delta_ref, sem):
     core = place[0]
     rows, cols = delta_ref.shape
     half = cols // 2
+    split = rows // 2
+    copies = [
+        pltpu.make_async_copy(
+            delta_hbm.at[pl.ds(i * split, split)], delta_ref.at[pl.ds(i * split, split)], sem.at[i]
+        )
+        for i in range(2)
+    ]
+    for copy in copies:
+        copy.start()
     row_index = place[3] + lax.broadcasted_iota(jnp.int32, (cols, RANK), 0)
     col_index = lax.broadcasted_iota(jnp.int32, (cols, RANK), 1)
     hashed = row_index * RANK + col_index + place[4]
@@ -92,18 +136,46 @@
     hashed = hashed ^ lax.shift_right_logical(hashed, jnp.int32(15))
     parity = lax.shift_right_logical(hashed, jnp.int32(11)) & 1
     signs = (2 * parity - 1).astype(F32).astype(BF)
-    delta = delta_ref[...].astype(BF)
-    part_ref[...] = dot(delta, signs).astype(BF).reshape(part_ref.shape)
-    left, right = delta[:, :half], delta[:, half:]
-    kept_ref[...] = jnp.where(core == 0, left, right)
-    sent_ref[:, :half] = jnp.where(core == 0, right, left)
-    spare = sent_ref.shape[1] - half
-    sent_ref[:, half:] = jnp.broadcast_to(tokens_ref[...].astype(F32), (rows, spare)).astype(BF)
+    for i, copy in enumerate(copies):
+        copy.wait()
+        span = slice(i * split, (i + 1) * split)
+        delta = delta_ref[span].astype(BF)
+        parts = part_ref.shape[0] // 2
+        part_ref[i * parts : (i + 1) * parts] = (
+            dot(delta, signs).astype(BF).reshape(parts, *part_ref.shape[1:])
+        )
+        left, right = delta[:, :half], delta[:, half:]
+        tokens = column(tokens_ref[i : i + 1].astype(F32))[:, : RANK // 2].astype(BF)
+        kept_ref[span] = jnp.concatenate([jnp.where(core == 0, left, right), tokens], axis=1)
+        sent_ref[span] = jnp.concatenate([jnp.where(core == 0, right, left), tokens], axis=1)
+
+
+def pool_kernel(place, up_hbm, pool_ref, gain_ref, gained_ref, up_out_ref, squares_ref, up_ref, sem):
+    z_half = place[1]
+    width = up_ref.shape[0]
+    first = pl.multiple_of(z_half * width, width)
+    copy = pltpu.make_async_copy(up_hbm.at[pl.ds(first, width)], up_ref, sem.at[0])
+    copy.start()
+    pool = jnp.where(z_half == 0, pool_ref[:, :width], pool_ref[:, width:]).astype(F32)
+    gain = jnp.where(z_half == 0, gain_ref[:, :width], gain_ref[:, width:])
+    gained = (pool * gain).astype(BF)
+    gained_ref[...] = gained
+    squares = jnp.broadcast_to(jnp.sum(pool * pool, axis=1, keepdims=True), (pool.shape[0], RANK))
+    hi, lo = hi_lo(squares)
+    squares_ref[0] = hi.astype(BF)
+    squares_ref[1] = lo.astype(BF)
+    copy.wait()
+    up_out_ref[...] = own_half(place, dot(gained, up_ref[...])).astype(BF)
+
+
+def spread_kernel(place, parts_ref, out_ref):
+    out_ref[...] = jnp.broadcast_to(total(parts_ref).astype(BF), out_ref.shape)
 
 
 def moved_kernel(place, basis_ref, kept_ref, got_ref, pool_ref, up_ref, squares_ref, out_ref):
     core = place[0]
-    rows, half = kept_ref.shape
+    rows, wide = kept_ref.shape
+    half = wide - RANK // 2
     count = basis_ref.shape[0] // 2
     own = basis_ref[pl.ds(core * count, count)].reshape(rows, RANK)
     other = basis_ref[pl.ds((1 - core) * count, count)].reshape(rows, RANK)
@@ -115,10 +187,10 @@
             *out_ref.shape[:2], values.shape[1]
         )
 
-    moved = dot_t(own, kept_ref[...]) + dot_t(other, got_ref[:, :half])
-    both = jnp.concatenate([moved.astype(BF), up_ref[...]], axis=1)
-    put(0, both)
-    put(2 * half, packed(dot_t(basis, basis), squares_ref[...], diagonal_offset(RANK, 0)))
+    moved = dot_t(own, kept_ref[...]) + dot_t(other, got_ref[...])
+    put(0, jnp.concatenate([moved[:, :half].astype(BF), up_ref[...]], axis=1))
+    squares = squares_ref[0].astype(F32) + squares_ref[1].astype(F32)
+    put(2 * half, packed(dot_t(basis, basis), squares, diagonal_offset(RANK, 0)))
     put(2 * half + RANK, dot(pool_ref[...], basis))
 
 
@@ -133,7 +205,15 @@
     out_ref[...] = jnp.broadcast_to(share.astype(BF), out_ref.shape)
 
 
-def first_kernel(place, z_ref, down_ref, step_ref, coef_ref, pre_ref):
+def down_copy(place, down_hbm, down_ref, sem):
+    half = down_ref.shape[0]
+    first = pl.multiple_of(place[0] * half, RANK // 2)
+    return pltpu.make_async_copy(down_hbm.at[pl.ds(first, half)], down_ref, sem.at[0])
+
+
+def first_kernel(place, down_hbm, z_ref, step_ref, coef_ref, pre_ref, down_ref, sem):
+    copy = down_copy(place, down_hbm, down_ref, sem)
+    copy.start()
     half = coef_ref.shape[1]
     gathered = z_ref[...].reshape(RANK, z_ref.shape[2])
     gram = gathered[:, 2 * half : 2 * half + RANK].astype(F32)
@@ -167,6 +247,7 @@
     pre = gathered[:, half : 2 * half].astype(F32) + dot(gathered[:, 2 * half + RANK :], coef)
     pre_ref[...] = pre.astype(BF)
     hidden = silu(pre * lax.rsqrt(squares / D + EPS)).astype(BF)
+    copy.wait()
     result = dot(hidden, down_ref[...]).astype(BF)
     count, rows, width = step_ref.shape
     step_ref[: count // 2] = result[:, :width].reshape(count // 2, rows, width)
@@ -174,11 +255,14 @@
 
 
 def second_kernel(
-    place, step_ref, pool_ref, gain_ref, up_ref, basis_ref, coef_ref, pick_ref, own_ref, out_ref, rows_ref
+    place, up_hbm, step_ref, pool_ref, gain_ref, basis_ref, coef_ref, kept_ref, got_ref, out_ref, rows_ref, up_ref, sem
 ):
     z_half = place[1]
     count, rows, width = step_ref.shape
     pool_rows = pool_ref.shape[0]
+    start = pl.multiple_of(z_half * width, width)
+    copy = pltpu.make_async_copy(up_hbm.at[pl.ds(start, width)], up_ref, sem.at[0])
+    copy.start()
     half = coef_ref.shape[1]
     basis = basis_ref[...].reshape(width, RANK)
     step = step_ref[...].astype(F32).reshape(2, pool_rows, width)
@@ -186,23 +270,33 @@
     left = (pool[:, :width].astype(F32) + step[0]).astype(BF)
     right = (pool[:, width:].astype(F32) + step[1]).astype(BF)
     carried = jnp.concatenate([left, right], axis=1)
-    gained = jnp.where(z_half == 0, left, right).astype(F32) * gain_ref[...]
-    gained = gained.astype(BF)
-    up = dot(gained, up_ref[...]) + dot(dot(gained, basis).astype(BF), coef_ref[...])
-
-    def second(pick):
-        return (dot(pick[0], carried) + dot(pick[1], pool)).astype(BF)
-
-    wide = second(pick_ref).astype(F32)
+    gain = jnp.where(z_half == 0, gain_ref[:, :width], gain_ref[:, width:])
+    gained = (jnp.where(z_half == 0, left, right).astype(F32) * gain).astype(BF)
+
+    def second(one, two):
+        return (dot(one, carried) + dot(two, pool)).astype(BF)
+
+    wide = second(
+        picks(place, kept_ref, got_ref, 0), picks(place, kept_ref, got_ref, 1)
+    ).astype(F32)
     squares = jnp.sum(wide * wide, axis=1, keepdims=True)
+    row = lax.broadcasted_iota(jnp.int32, (rows_ref.shape[0], pool_rows), 0)
+    lane = lax.broadcasted_iota(jnp.int32, (rows_ref.shape[0], pool_rows), 1)
+    here = jnp.where(lane == row + place[5], 1.0, 0.0).astype(BF)
+    tokens = kept_ref[:, half : half + 1]
+    rows_ref[...] = second(
+        dot(here, chosen(tokens, 0)).astype(BF), dot(here, chosen(tokens, 1)).astype(BF)
+    )
     lane = lax.broadcasted_iota(jnp.int32, (pool_rows, out_ref.shape[2] - half), 1)
     first = 4 * z_half
     tail = jnp.zeros(lane.shape, F32)
     for place_in, value in enumerate((*hi_lo(squares[:pool_rows]), *hi_lo(squares[pool_rows:]))):
         tail = jnp.where(lane == first + place_in, value, tail)
+    low = dot(dot(gained, basis).astype(BF), coef_ref[...])
+    copy.wait()
+    up = own_half(place, dot(gained, up_ref[...])) + low
     both = jnp.concatenate([up.astype(BF), tail.astype(BF)], axis=1)
     out_ref[...] = both.reshape(out_ref.shape)
-    rows_ref[...] = second(own_ref)
 
 
 def second_share_kernel(half, place, parts_ref, out_ref):
@@ -216,7 +310,9 @@
     out_ref[...] = jnp.broadcast_to(out.astype(BF), out_ref.shape)
 
 
-def last_kernel(place, z_ref, pre_ref, pick_ref, down_ref, out_ref):
+def last_kernel(place, down_hbm, z_ref, pre_ref, kept_ref, got_ref, out_ref, down_ref, sem):
+    copy = down_copy(place, down_hbm, down_ref, sem)
+    copy.start()
     z_half = place[1]
     half = pre_ref.shape[1]
     pool_rows = pre_ref.shape[0]
@@ -229,14 +325,14 @@
         return jnp.sum(jnp.where(chosen, gathered.astype(F32), 0.0), axis=1, keepdims=True)
 
     scale = lax.rsqrt(jnp.concatenate([squares(0), squares(2)], axis=0) / D + EPS)
-    pre = dot(pick_ref[0], gathered[:, :half]) + dot(pick_ref[1], pre_ref[...])
+    one, two = picks(place, kept_ref, got_ref, 0), picks(place, kept_ref, got_ref, 1)
+    pre = dot(one, gathered[:, :half]) + dot(two, pre_ref[...])
     hidden = silu(pre * scale).astype(BF)
+    copy.wait()
     out_ref[...] = dot(hidden, down_ref[...]).astype(BF).reshape(out_ref.shape)
 
 
 def local(weight_delta, sketch_seed, up_weight, down_weight, norm_gain, state_pool, token_rows):
-    core = lax.axis_index("c")
-    z_half = lax.axis_index("zh")
     learner = lax.axis_index(L)
     rows, cols = weight_delta.shape
     half = cols // 2
@@ -244,62 +340,59 @@
     count = state_pool.shape[0]
     out_rows = count // 16
     place = jnp.stack(
-        [core, z_half, lax.axis_index(Z), learner * cols, sketch_seed[0] * 7919]
+        [
+            lax.axis_index("c"),
+            lax.axis_index("zh"),
+            lax.axis_index(Z),
+            learner * cols,
+            sketch_seed[0] * 7919,
+            learner * out_rows,
+        ]
     ).astype(jnp.int32)
-
-    tokens = token_rows[:, 0, :]
+    padded = half + RANK // 2
     part, kept, sent = call(
         range_kernel,
-        ((16, rows // 16, RANK), (rows, half), (rows, half + 64)),
+        ((16, rows // 16, RANK), (rows, padded), (rows, padded)),
         place,
-        weight_delta,
-        tokens.reshape(-1, 1),
+        token_rows[:, 0, :],
+        hbm=weight_delta,
+        scratch=(pltpu.VMEM((rows, cols), F32),),
     )
     received = lax.ppermute(sent, "c", [(0, 1), (1, 0)])
     parts = swap(part, L)
-
-    def own_half(x):
-        return jnp.where(core == 0, x[:, :half], x[:, half:])
-
-    pool_half = lax.dynamic_slice_in_dim(state_pool, z_half * width, width, 1).astype(F32)
-    gain_half = lax.dynamic_slice_in_dim(norm_gain, z_half * width, width, 0).astype(F32)[None]
-    up_own = own_half(lax.dynamic_slice_in_dim(up_weight, z_half * width, width, 0))
-    down_own = lax.dynamic_slice_in_dim(down_weight, core * half, half, 0)
-    pool_gained = (pool_half * gain_half).astype(BF)
-    pool_up = dot(pool_gained, up_own).astype(BF)
-    squares = jnp.sum(pool_half * pool_half, axis=1, keepdims=True)
-    mine = tokens[:, :, None]
-    theirs = received[:, half : half + 1].astype(jnp.int32).reshape(2, count, 1)
-    both = jnp.where(
-        core == 0, jnp.concatenate([mine, theirs], 1), jnp.concatenate([theirs, mine], 1)
-    )
-    picks = (both == lax.broadcasted_iota(jnp.int32, (2, 2 * count, count), 2)).astype(BF)
-    own = lax.dynamic_slice_in_dim(mine, learner * out_rows, out_rows, 1)
-    own_picks = (own == lax.broadcasted_iota(jnp.int32, (2, out_rows, count), 2)).astype(BF)
-
-    range_share = jnp.sum(parts.astype(F32), axis=0).astype(BF)
-    side = (kept, received, pool_gained, pool_up, squares, gain_half, up_own, down_own, picks, own_picks, place, state_pool)
-    range_share, side = lax.optimization_barrier((range_share, side))
-    kept, received, pool_gained, pool_up, squares, gain_half, up_own, down_own, picks, own_picks, place, pool = side
-
-    basis = sent_to_all(range_share, CL)
+    gain = norm_gain.astype(F32)[None]
+    up_scratch = (pltpu.VMEM((width, cols), BF),)
+    down_scratch = (pltpu.VMEM((half, 2 * width), BF),)
+    gained, pool_up, squares = call(
+        pool_kernel,
+        ((count, width), (count, half), (2, count, RANK)),
+        place, state_pool, gain,
+        hbm=up_weight, scratch=up_scratch,
+    )
+    parts, received, gained, pool_up, squares, kept, place, gain, pool = lax.optimization_barrier(
+        (parts, received, gained, pool_up, squares, kept, place, gain, state_pool)
+    )
+    (spread,) = call(spread_kernel, ((32, rows // 16, RANK),), place, parts)
+    basis = swap(spread, CL)
     (stacked,) = call(
         moved_kernel,
         ((16, count // 16, 2 * half + 2 * RANK),),
-        place, basis, kept, received, pool_gained, pool_up, squares,
+        place, basis, kept, received, gained, pool_up, squares,
     )
     (share,) = call(share_kernel, (stacked.shape,), place, swap(stacked, Z))
     step_part, coef, pool_pre = call(
         first_kernel,
         ((32, count // 16, width), (RANK, half), (count, half)),
-        place, swap(share, Z), down_own,
-    )
-    step_share = jnp.sum(swap(step_part, CL).astype(F32), axis=0).astype(BF)
-    step = sent_to_all(step_share, CL)
+        place, swap(share, Z),
+        hbm=down_weight, scratch=down_scratch,
+    )
+    (spread,) = call(spread_kernel, (step_part.shape,), place, swap(step_part, CL))
+    step = swap(spread, CL)
     stacked, own_second = call(
         second_kernel,
-        ((16, count // 16, half + 64), (out_rows, 2 * width)),
-        place, step, pool, gain_half, up_own, basis, coef, picks, own_picks,
+        ((16, count // 16, padded), (out_rows, 2 * width)),
+        place, step, pool, gain, basis, coef, kept, received,
+        hbm=up_weight, scratch=up_scratch,
     )
     (share,) = call(
         functools.partial(second_share_kernel, half), (stacked.shape,), place, swap(stacked, Z)
@@ -307,7 +400,8 @@
     (last,) = call(
         last_kernel,
         ((32, out_rows, 2 * width),),
-        place, swap(share, Z), pool_pre, picks, down_own,
+        place, swap(share, Z), pool_pre, kept, received,
+        hbm=down_weight, scratch=down_scratch,
     )
     last_share = jnp.sum(swap(last, CL).astype(F32), axis=0)
     return (own_second.astype(F32) + last_share).astype(BF)[None]

time: 197 us -> 187 us (0.949)
  blocking collectives: 137 us -> 149 us
  starting transfers between devices: 19.6 us -> 12.2 us
  local copies, waits for them, and re-layouts: 11.6 us -> 4.41 us
  other arithmetic: 7.51 us -> 1.38 us
  waiting for transfers between devices: 6.8 us -> 2.28 us
  Pallas kernels: 11.9 us -> 16.1 us
    all_to_all x7 -> x8, blocking collectives: 137 us -> 149 us  [swap(): return lax.all_to_all(x, axis, split_axis=0, concat_axis=0, tiled=True)]
    all_to_all x2 -> x1, starting transfers between devices: 14.9 us -> 3.5 us  [swap(): return lax.all_to_all(x, axis, split_axis=0, concat_axis=0, tiled=True)]
    all_to_all x2 -> x1, waiting for transfers between devices: 6.8 us -> 2.28 us  [swap(): return lax.all_to_all(x, axis, split_axis=0, concat_axis=0, tiled=True)]
    pallas_call x7 -> x10, Pallas kernels: 11.9 us -> 16.1 us  [call(): pl.pallas_call(kernel, out_shape=tuple((jax.ShapeDtypeStruct(shape, BF) f...]
    ppermute x1, starting transfers between devices: 4.66 us -> 8.75 us  [local(): received = lax.ppermute(sent, 'c', [(0, 1), (1, 0)])]
    unnamed x26 -> x14, local copies, waits for them, and re-layouts: 7.73 us -> 4.32 us
    reduce_sum x3 -> x0, other arithmetic: 2.65 us -> none  [the longest x1 1.6 us: local(): step_share = jnp.sum(swap(step_part, CL).astype(F32), axis=0).astype(BF)]
  transfers between devices with their start and end apart: 3 -> 2, of which waited for: 1 -> 1; matrix products, arithmetic and copies ran while one was open for 3% -> 0% of each run, Pallas kernels for 0% -> 1%
where the time goes in v3:
time: 187 us; the launch traced here: 186 us
  blocking collectives  149 us (80%)
  Pallas kernels  16.1 us (9%)
  starting transfers between devices  12.2 us (7%)
  local copies, waits for them, and re-layouts  4.41 us (2%)
  waiting for transfers between devices  2.28 us (1%)
    all_to_all x8, blocking collectives, swap(): return lax.all_to_all(x, axis, split_axis=0, concat_axis=0, tiled=True)  149 us
    pallas_call x10, Pallas kernels, call(): pl.pallas_call(kernel, out_shape=tuple((jax.ShapeDtypeStruct(shape, BF) f...  16.1 us
    ppermute x1, starting transfers between devices, local(): received = lax.ppermute(sent, 'c', [(0, 1), (1, 0)])  8.75 us
    unnamed x14, local copies, waits for them, and re-layouts  4.32 us
  transfers between devices with their start and end apart: 2, of which 1 were waited for; matrix products, arithmetic and copies ran while one was open for 0% of the time, Pallas kernels for 1%

profile of v3, /device:TPU:1, one launch (start us, length us, event | category | flops | bytes accessed | tf_op | source)
XLA Modules:
  0.0 186.4 jit_solution(11016174235473197408)
XLA Ops:
  0.7 0.1 stack.24.place
  0.7 1.2 copy-done.5
  1.9 0.7 copy-done.6
  2.6 2.6 %shard_map.73 = (bf16[16,16,128]{2,1,0:T(8,128)(2,1)}, bf16[256,512]{1,0:T(8,128)(2,1)S(1)}, bf16[256,512]{1,0:T(8,128)(2,1)S(1)}) custom-call(s32[6]{0:T(128)S(1)} %stack.24.place, f32[256,896]{1,0:T(8,128)S(1)} %copy-done.5, s32[2,128]{1,0:T(2,128)S(1)} %bitcast.11), custom_call_target="tpu_custom_call" | custom-call | tf_op jit(solution)/shard_map/pallas_call | solution.py:81
  5.2 8.7 %collective-permute-start = (bf16[256,512]{1,0:T(8,128)(2,1)S(1)}, bf16[256,512]{1,0:T(8,128)(2,1)S(1)}, u32[]{:S(2)}, u32[]{:S(2)}) collective-permute-start(bf16[256,512]{1,0:T(8,128)(2,1)S(1)} %get-tuple-element.26), channel_id=1, source_target_pairs={{0,1},{1,0},{2,3},{3,2},{4,5},{5,4},{6,7},{7,6},{8,9},{9,8},{10,11... | collective-permute-start | bytes 786440 | tf_op jit(solution)/shard_map/ppermute | solution.py:361
  13.9 3.5 %all-to-all-start = ((bf16[16,16,128]{2,1,0:T(8,128)(2,1)}), bf16[16,16,128]{2,1,0:T(8,128)(2,1)S(1)}, u32[]{:S(2)}, u32[]{:S(2)}) async-start(bf16[16,16,128]{2,1,0:T(8,128)(2,1)} %get-tuple-element.25), calls=%async_computation | async-start | bytes 131072 | tf_op jit(solution)/shard_map/all_to_all | solution.py:22
  17.4 0.7 broadcast_in_dim.11
  18.1 1.5 copy-done
  19.6 0.9 copy-done.3
  20.6 1.3 shard_map.74
  21.9 0.0 copy-start.2
  21.9 2.3 %all-to-all-done.parts_ref = bf16[16,16,128]{2,1,0:T(8,128)(2,1)S(1)} async-done(((bf16[16,16,128]{2,1,0:T(8,128)(2,1)}), bf16[16,16,128]{2,1,0:T(8,128)(2,1)S(1)}, u32[]{:S(2)}, u32[]{:S(2)}) %all-to-all-start) | async-done | bytes 65568 | tf_op jit(solution)/shard_map/all_to_all | solution.py:22
  24.2 0.0 collective-permute-done.got_ref
  24.2 0.6 shard_map.75
  24.8 12.3 %all_to_all.45.basis_ref = bf16[32,16,128]{2,1,0:T(8,128)(2,1)S(1)} all-to-all(bf16[32,16,128]{2,1,0:T(8,128)(2,1)S(1)} %shard_map.75), channel_id=1, replica_groups=mesh['y'=4,'x'=4,'zl'=8,'zh'=2,'c'=2] {'c','y','x'}, dimensions={0} | all-to-all | bytes 262144 | tf_op jit(solution)/shard_map/all_to_all | solution.py:22
  37.1 0.9 shard_map.76
  37.9 30.9 %all_to_all.46.parts_ref = bf16[16,8,1152]{2,1,0:T(8,128)(2,1)S(1)} all-to-all(bf16[16,8,1152]{2,1,0:T(8,128)(2,1)S(1)} %shard_map.76), channel_id=1, replica_groups=mesh['y'=4,'x'=4,'zl'=8,'zh'=2,'c'=2] {'zl','zh'}, dimensions={0} | all-to-all | bytes 589824 | tf_op jit(solution)/shard_map/all_to_all | solution.py:22
  68.9 0.7 shard_map.77
  69.5 23.6 %all_to_all.47.z_ref = bf16[16,8,1152]{2,1,0:T(8,128)(2,1)S(1)} all-to-all(bf16[16,8,1152]{2,1,0:T(8,128)(2,1)S(1)} %shard_map.77), channel_id=1, replica_groups=mesh['y'=4,'x'=4,'zl'=8,'zh'=2,'c'=2] {'zl','zh'}, dimensions={0} | all-to-all | bytes 589824 | tf_op jit(solution)/shard_map/all_to_all | solution.py:22
  93.1 5.2 %shard_map.78 = (bf16[32,8,512]{2,1,0:T(8,128)(2,1)S(1)}, bf16[128,448]{1,0:T(8,128)(2,1)S(1)}, bf16[128,448]{1,0:T(8,128)(2,1)S(1)}) custom-call(s32[6]{0:T(128)S(1)} %stack.24.place, bf16[896,1024]{1,0:T(8,128)(2,1)S(1)} %copy-done.2, bf16[16,8,1152]{2,1,0:T(8,128)(2,1)S(1)} %all_to_all.47.z_ref), custom_call_target="tpu_custom_call" | custom-call | tf_op jit(solution)/shard_map/pallas_call | solution.py:81
  98.3 17.0 %all_to_all.48.parts_ref = bf16[32,8,512]{2,1,0:T(8,128)(2,1)S(1)} all-to-all(bf16[32,8,512]{2,1,0:T(8,128)(2,1)S(1)} %get-tuple-element.38), channel_id=1, replica_groups=mesh['y'=4,'x'=4,'zl'=8,'zh'=2,'c'=2] {'c','y','x'}, dimensions={0} | all-to-all | bytes 524288 | tf_op jit(solution)/shard_map/all_to_all | solution.py:22
  115.3 0.6 shard_map.79
  115.9 12.4 %all_to_all.49.step_ref = bf16[32,8,512]{2,1,0:T(8,128)(2,1)S(1)} all-to-all(bf16[32,8,512]{2,1,0:T(8,128)(2,1)S(1)} %shard_map.79), channel_id=1, replica_groups=mesh['y'=4,'x'=4,'zl'=8,'zh'=2,'c'=2] {'c','y','x'}, dimensions={0} | all-to-all | bytes 524288 | tf_op jit(solution)/shard_map/all_to_all | solution.py:22
  128.3 0.0 copy-done.4
  128.3 2.0 %shard_map.80 = (bf16[16,8,512]{2,1,0:T(8,128)(2,1)S(1)}, bf16[8,1024]{1,0:T(8,128)(2,1)S(1)}) custom-call(s32[6]{0:T(128)S(1)} %stack.24.place, bf16[1024,896]{1,0:T(8,128)(2,1)S(1)} %copy-done.1, bf16[32,8,512]{2,1,0:T(8,128)(2,1)S(1)} %all_to_all.49.step_ref, bf16[128,1024]{1,0:T(8,128)(2,1)S(1)} %copy-done.4, f32[1,1024]{1,0:T(1,128)S(1)} %bitcast.10, ...), custom_call_target="tpu_custom_call" | custom-call | tf_op jit(solution)/shard_map/pallas_call | solution.py:81
  130.3 17.7 %all_to_all.50.parts_ref = bf16[16,8,512]{2,1,0:T(8,128)(2,1)S(1)} all-to-all(bf16[16,8,512]{2,1,0:T(8,128)(2,1)S(1)} %get-tuple-element.43), channel_id=1, replica_groups=mesh['y'=4,'x'=4,'zl'=8,'zh'=2,'c'=2] {'zl','zh'}, dimensions={0} | all-to-all | bytes 262144 | tf_op jit(solution)/shard_map/all_to_all | solution.py:22
  148.0 0.6 shard_map.81
  148.7 17.6 %all_to_all.51.z_ref = bf16[16,8,512]{2,1,0:T(8,128)(2,1)S(1)} all-to-all(bf16[16,8,512]{2,1,0:T(8,128)(2,1)S(1)} %shard_map.81), channel_id=1, replica_groups=mesh['y'=4,'x'=4,'zl'=8,'zh'=2,'c'=2] {'zl','zh'}, dimensions={0} | all-to-all | bytes 262144 | tf_op jit(solution)/shard_map/all_to_all | solution.py:22
  166.2 1.7 shard_map.82
  167.9 17.8 %all_to_all.52 = bf16[32,8,1024]{2,1,0:T(8,128)(2,1)S(1)} all-to-all(bf16[32,8,1024]{2,1,0:T(8,128)(2,1)S(1)} %shard_map.82), channel_id=1, replica_groups=mesh['y'=4,'x'=4,'zl'=8,'zh'=2,'c'=2] {'c','y','x'}, dimensions={0} | all-to-all | bytes 1048576 | tf_op jit(solution)/shard_map/all_to_all | solution.py:22
  185.7 0.1 convert_reduce_fusion
  185.8 0.6 fusion
  (8 shorter events, 0.0 us)
Async XLA Ops:
  0.7 1.2 copy-start.5
  1.9 0.7 copy-start.6
  5.2 19.0 %collective-permute-start = (bf16[256,512]{1,0:T(8,128)(2,1)S(1)}, bf16[256,512]{1,0:T(8,128)(2,1)S(1)}, u32[]{:S(2)}, u32[]{:S(2)}) collective-permute-start(bf16[256,512]{1,0:T(8,128)(2,1)S(1)} %get-tuple-element.26), channel_id=1, source_target_pairs={{0,1},{1,0},{2,3},{3,2},{4,5},{5,4},{6,7},{7,6},{8,9},{9,8},{10,11... | collective-permute-start | bytes 786440 | tf_op jit(solution)/shard_map/ppermute | solution.py:361
  13.9 10.3 %all-to-all-start = ((bf16[16,16,128]{2,1,0:T(8,128)(2,1)}), bf16[16,16,128]{2,1,0:T(8,128)(2,1)S(1)}, u32[]{:S(2)}, u32[]{:S(2)}) async-start(bf16[16,16,128]{2,1,0:T(8,128)(2,1)} %get-tuple-element.25), calls=%async_computation | async-start | bytes 131072 | tf_op jit(solution)/shard_map/all_to_all | solution.py:22
  18.1 1.5 copy-start
  19.6 0.9 copy-start.3
  21.9 71.2 %copy-start.2 = (bf16[896,1024]{1,0:T(8,128)(2,1)S(1)}, bf16[896,1024]{1,0:T(8,128)(2,1)}, u32[]{:S(2)}) copy-start(bf16[896,1024]{1,0:T(8,128)(2,1)} %down_hbm.3) | copy-start | bytes 5505028
  93.1 35.1 %copy-start.1 = (bf16[1024,896]{1,0:T(8,128)(2,1)S(1)}, bf16[1024,896]{1,0:T(8,128)(2,1)}, u32[]{:S(2)}) copy-start(bf16[1024,896]{1,0:T(8,128)(2,1)} %up_hbm.3) | copy-start | bytes 5505028
  93.1 35.1 %copy-start.4 = (bf16[128,1024]{1,0:T(8,128)(2,1)S(1)}, bf16[128,1024]{1,0:T(8,128)(2,1)}, u32[]{:S(2)}) copy-start(bf16[128,1024]{1,0:T(8,128)(2,1)} %pool_ref.2) | copy-start | bytes 786436

commit v4 on v3

--- a/solution.py
+++ b/solution.py
@@ -7,6 +7,7 @@
 from jax.experimental.pallas import tpu as pltpu
 from jax.sharding import Mesh
 from jax.sharding import PartitionSpec as P
+
 
 D = 8192
 RANK = 128
@@ -22,10 +23,6 @@
     return lax.all_to_all(x, axis, split_axis=0, concat_axis=0, tiled=True)
 
 
-def sent_to_all(x, axis):
-    return swap(jnp.broadcast_to(x, (lax.axis_size(axis), *x.shape)), axis)
-
-
 def dot(a, b):
     return jnp.dot(a, b, preferred_element_type=F32)
 
@@ -71,7 +68,7 @@
 VMEM = pl.BlockSpec(memory_space=pltpu.VMEM)
 
 
-def call(kernel, shapes, place, *arrays, hbm=None, scratch=()):
+def call(kernel, shapes, place, *arrays, hbm=None, scratch=(), limit=16):
     specs = [pl.BlockSpec(memory_space=pltpu.SMEM)]
     if hbm is not None:
         arrays = (hbm, *arrays)
@@ -84,7 +81,7 @@
         in_specs=specs,
         out_specs=(VMEM,) * len(shapes),
         scratch_shapes=scratch,
-        compiler_params=pltpu.CompilerParams(vmem_limit_bytes=16 * 1024 * 1024),
+        compiler_params=pltpu.CompilerParams(vmem_limit_bytes=int(limit * 1024 * 1024)),
     )(place, *arrays)
 
 
@@ -114,10 +111,8 @@
     return jnp.where(place[0] == 0, x[:, :half], x[:, half:])
 
 
-def range_kernel(place, delta_hbm, tokens_ref, part_ref, kept_ref, sent_ref, delta_ref, sem):
-    core = place[0]
+def range_kernel(place, delta_hbm, part_ref, delta_ref, sem):
     rows, cols = delta_ref.shape
-    half = cols // 2
     split = rows // 2
     copies = [
         pltpu.make_async_copy(
@@ -136,28 +131,33 @@
     hashed = hashed ^ lax.shift_right_logical(hashed, jnp.int32(15))
     parity = lax.shift_right_logical(hashed, jnp.int32(11)) & 1
     signs = (2 * parity - 1).astype(F32).astype(BF)
+    parts = part_ref.shape[0] // 2
     for i, copy in enumerate(copies):
         copy.wait()
-        span = slice(i * split, (i + 1) * split)
-        delta = delta_ref[span].astype(BF)
-        parts = part_ref.shape[0] // 2
-        part_ref[i * parts : (i + 1) * parts] = (
-            dot(delta, signs).astype(BF).reshape(parts, *part_ref.shape[1:])
+        product = dot(delta_ref[i * split : (i + 1) * split].astype(BF), signs)
+        part_ref[i * parts : (i + 1) * parts] = product.astype(BF).reshape(
+            parts, *part_ref.shape[1:]
         )
-        left, right = delta[:, :half], delta[:, half:]
-        tokens = column(tokens_ref[i : i + 1].astype(F32))[:, : RANK // 2].astype(BF)
-        kept_ref[span] = jnp.concatenate([jnp.where(core == 0, left, right), tokens], axis=1)
-        sent_ref[span] = jnp.concatenate([jnp.where(core == 0, right, left), tokens], axis=1)
-
-
-def pool_kernel(place, up_hbm, pool_ref, gain_ref, gained_ref, up_out_ref, squares_ref, up_ref, sem):
+
+
+def pool_kernel(
+    place, up_hbm, delta_ref, tokens_ref, pool_ref, gain_ref, gained_ref, up_out_ref, squares_ref, kept_ref, sent_ref, up_ref, sem
+):
+    core = place[0]
     z_half = place[1]
     width = up_ref.shape[0]
     first = pl.multiple_of(z_half * width, width)
     copy = pltpu.make_async_copy(up_hbm.at[pl.ds(first, width)], up_ref, sem.at[0])
     copy.start()
+    delta = delta_ref[...].astype(BF)
+    half = delta.shape[1] // 2
+    left, right = delta[:, :half], delta[:, half:]
+    tokens = jnp.concatenate([column(tokens_ref[i : i + 1].astype(F32)) for i in range(2)], axis=0)
+    tokens = tokens[:, : RANK // 2].astype(BF)
+    kept_ref[...] = jnp.concatenate([jnp.where(core == 0, left, right), tokens], axis=1)
+    sent_ref[...] = jnp.concatenate([jnp.where(core == 0, right, left), tokens], axis=1)
     pool = jnp.where(z_half == 0, pool_ref[:, :width], pool_ref[:, width:]).astype(F32)
-    gain = jnp.where(z_half == 0, gain_ref[:, :width], gain_ref[:, width:])
+    gain = jnp.where(z_half == 0, gain_ref[:, :width].astype(F32), gain_ref[:, width:].astype(F32))
     gained = (pool * gain).astype(BF)
     gained_ref[...] = gained
     squares = jnp.broadcast_to(jnp.sum(pool * pool, axis=1, keepdims=True), (pool.shape[0], RANK))
@@ -238,11 +238,13 @@
     def refine(state):
         count, _, inverse = state
         left = eye - precise(unit, inverse)
-        return count + 1, jnp.sum(left * left), inverse + precise(inverse, left)
+        moved = dot(inverse.astype(BF), left.astype(BF))
+        return count + 1, jnp.sum(left * left), inverse + moved
 
     _, _, inverse = lax.while_loop(going, refine, (0, jnp.float32(1.0), start))
-    moved = gathered[:, :half].astype(F32) * scale_col
-    coef = (precise(inverse, moved) * scale_col).astype(BF)
+    hi, lo = hi_lo(inverse * scale_col * scale_row)
+    moved = gathered[:, :half]
+    coef = (dot(hi.astype(BF), moved) + dot(lo.astype(BF), moved)).astype(BF)
     coef_ref[...] = coef
     pre = gathered[:, half : 2 * half].astype(F32) + dot(gathered[:, 2 * half + RANK :], coef)
     pre_ref[...] = pre.astype(BF)
@@ -258,7 +260,7 @@
     place, up_hbm, step_ref, pool_ref, gain_ref, basis_ref, coef_ref, kept_ref, got_ref, out_ref, rows_ref, up_ref, sem
 ):
     z_half = place[1]
-    count, rows, width = step_ref.shape
+    _, _, width = step_ref.shape
     pool_rows = pool_ref.shape[0]
     start = pl.multiple_of(z_half * width, width)
     copy = pltpu.make_async_copy(up_hbm.at[pl.ds(start, width)], up_ref, sem.at[0])
@@ -270,7 +272,7 @@
     left = (pool[:, :width].astype(F32) + step[0]).astype(BF)
     right = (pool[:, width:].astype(F32) + step[1]).astype(BF)
     carried = jnp.concatenate([left, right], axis=1)
-    gain = jnp.where(z_half == 0, gain_ref[:, :width], gain_ref[:, width:])
+    gain = jnp.where(z_half == 0, gain_ref[:, :width].astype(F32), gain_ref[:, width:].astype(F32))
     gained = (jnp.where(z_half == 0, left, right).astype(F32) * gain).astype(BF)
 
     def second(one, two):
@@ -332,7 +334,7 @@
     out_ref[...] = dot(hidden, down_ref[...]).astype(BF).reshape(out_ref.shape)
 
 
-def local(weight_delta, sketch_seed, up_weight, down_weight, norm_gain, state_pool, token_rows):
+def staged(weight_delta, sketch_seed, up_weight, down_weight, norm_gain, state_pool, token_rows):
     learner = lax.axis_index(L)
     rows, cols = weight_delta.shape
     half = cols // 2
@@ -350,25 +352,25 @@
         ]
     ).astype(jnp.int32)
     padded = half + RANK // 2
-    part, kept, sent = call(
+    (part,) = call(
         range_kernel,
-        ((16, rows // 16, RANK), (rows, padded), (rows, padded)),
+        ((16, rows // 16, RANK),),
         place,
-        token_rows[:, 0, :],
         hbm=weight_delta,
         scratch=(pltpu.VMEM((rows, cols), F32),),
-    )
-    received = lax.ppermute(sent, "c", [(0, 1), (1, 0)])
+        limit=63.5,
+    )
     parts = swap(part, L)
-    gain = norm_gain.astype(F32)[None]
+    gain = norm_gain[None]
     up_scratch = (pltpu.VMEM((width, cols), BF),)
     down_scratch = (pltpu.VMEM((half, 2 * width), BF),)
-    gained, pool_up, squares = call(
+    gained, pool_up, squares, kept, sent = call(
         pool_kernel,
-        ((count, width), (count, half), (2, count, RANK)),
-        place, state_pool, gain,
-        hbm=up_weight, scratch=up_scratch,
-    )
+        ((count, width), (count, half), (2, count, RANK), (rows, padded), (rows, padded)),
+        place, weight_delta, token_rows[:, 0, :], state_pool, gain,
+        hbm=up_weight, scratch=up_scratch, limit=16,
+    )
+    received = lax.ppermute(sent, "c", [(0, 1), (1, 0)])
     parts, received, gained, pool_up, squares, kept, place, gain, pool = lax.optimization_barrier(
         (parts, received, gained, pool_up, squares, kept, place, gain, state_pool)
     )
@@ -412,7 +414,7 @@
         mesh.devices.reshape(4, 4, mesh.shape["rollout"], 2, 2), ("y", "x", "zl", "zh", "c")
     )
     return jax.shard_map(
-        local,
+        staged,
         mesh=torus,
         in_specs=(
             P(("zl", "zh", "c"), L),

time: 187 us -> 194 us (1.037)
  blocking collectives: 149 us -> 159 us
  starting transfers between devices: 12.2 us -> 8.74 us
  local copies, waits for them, and re-layouts: 4.41 us -> 7.28 us
  waiting for transfers between devices: 2.28 us -> 0.01 us
    all_to_all x8 -> x9, blocking collectives: 149 us -> 159 us  [swap(): return lax.all_to_all(x, axis, split_axis=0, concat_axis=0, tiled=True)]
    all_to_all x1 -> x0, starting transfers between devices: 3.5 us -> none  [swap(): return lax.all_to_all(x, axis, split_axis=0, concat_axis=0, tiled=True)]
    all_to_all x1 -> x0, waiting for transfers between devices: 2.28 us -> none  [swap(): return lax.all_to_all(x, axis, split_axis=0, concat_axis=0, tiled=True)]
    unnamed x14 -> x26, local copies, waits for them, and re-layouts: 4.32 us -> 6.51 us
  transfers between devices with their start and end apart: 2 -> 1, of which waited for: 1 -> 0; matrix products, arithmetic and copies ran while one was open for 0% -> 0% of each run, Pallas kernels for 1% -> 1%
where the time goes in v4:
time: 194 us
  blocking collectives  159 us (82%)
  Pallas kernels  17.3 us (9%)
  starting transfers between devices  8.74 us (5%)
  local copies, waits for them, and re-layouts  7.28 us (4%)
    all_to_all x9, blocking collectives, swap(): return lax.all_to_all(x, axis, split_axis=0, concat_axis=0, tiled=True)  159 us
    pallas_call x10, Pallas kernels, call(): pl.pallas_call(kernel, out_shape=tuple((jax.ShapeDtypeStruct(shape, BF) f...  17.3 us
    ppermute x1, starting transfers between devices, staged(): received = lax.ppermute(sent, 'c', [(0, 1), (1, 0)])  8.74 us
    unnamed x26, local copies, waits for them, and re-layouts  6.51 us
  transfers between devices with their start and end apart: 1, of which 0 were waited for; matrix products, arithmetic and copies ran while one was open for 0% of the time, Pallas kernels for 1%

profile of v4, /device:TPU:1, one launch (start us, length us, event | category | flops | bytes accessed | tf_op | source)
XLA Modules:
  0.0 193.6 jit_solution(8598696172131029941)
XLA Ops:
  0.7 0.7 broadcast_in_dim.6.gain_ref
  1.3 0.1 stack.24.place
  1.4 1.5 copy-done
  2.9 1.2 copy-done.3
  4.1 0.9 copy-done.4
  5.1 0.7 copy-done.12
  5.7 1.9 shard_map.74
  7.6 0.6 copy-done.6
  8.3 8.7 %collective-permute-start = (bf16[256,512]{1,0:T(8,128)(2,1)}, bf16[256,512]{1,0:T(8,128)(2,1)}, u32[]{:S(2)}, u32[]{:S(2)}) collective-permute-start(bf16[256,512]{1,0:T(8,128)(2,1)} %get-tuple-element.24), channel_id=1, source_target_pairs={{0,1},{1,0},{2,3},{3,2},{4,5},{5,4},{6,7},{7,6},{8,9},{9,8},{10,11... | collective-permute-start | bytes 786440 | tf_op jit(solution)/shard_map/ppermute | solution.py:373
  17.0 2.8 %shard_map.73 = bf16[16,16,128]{2,1,0:T(8,128)(2,1)} custom-call(s32[6]{0:T(128)} %copy-done.8, f32[256,896]{1,0:T(8,128)} %delta_ref.1), custom_call_target="tpu_custom_call" | custom-call | tf_op jit(solution)/shard_map/pallas_call | solution.py:78
  19.8 0.0 copy-start.2
  19.8 10.4 %all_to_all.45.parts_ref = bf16[16,16,128]{2,1,0:T(8,128)(2,1)S(1)} all-to-all(bf16[16,16,128]{2,1,0:T(8,128)(2,1)} %shard_map.73), channel_id=1, replica_groups=mesh['y'=4,'x'=4,'zl'=8,'zh'=2,'c'=2] {'y','x'}, dimensions={0} | all-to-all | bytes 131072 | tf_op jit(solution)/shard_map/all_to_all | solution.py:23
  30.2 0.6 copy-done.9
  30.8 0.6 shard_map.75
  31.4 11.6 %all_to_all.46.basis_ref = bf16[32,16,128]{2,1,0:T(8,128)(2,1)S(1)} all-to-all(bf16[32,16,128]{2,1,0:T(8,128)(2,1)S(1)} %shard_map.75), channel_id=1, replica_groups=mesh['y'=4,'x'=4,'zl'=8,'zh'=2,'c'=2] {'c','y','x'}, dimensions={0} | all-to-all | bytes 262144 | tf_op jit(solution)/shard_map/all_to_all | solution.py:23
  43.0 0.9 copy-done.7
  43.9 1.3 shard_map.76
  45.2 30.8 %all_to_all.47.parts_ref = bf16[16,8,1152]{2,1,0:T(8,128)(2,1)S(1)} all-to-all(bf16[16,8,1152]{2,1,0:T(8,128)(2,1)S(1)} %shard_map.76), channel_id=1, replica_groups=mesh['y'=4,'x'=4,'zl'=8,'zh'=2,'c'=2] {'zl','zh'}, dimensions={0} | all-to-all | bytes 589824 | tf_op jit(solution)/shard_map/all_to_all | solution.py:23
  76.0 0.7 shard_map.77
  76.6 23.7 %all_to_all.48.z_ref = bf16[16,8,1152]{2,1,0:T(8,128)(2,1)S(1)} all-to-all(bf16[16,8,1152]{2,1,0:T(8,128)(2,1)S(1)} %shard_map.77), channel_id=1, replica_groups=mesh['y'=4,'x'=4,'zl'=8,'zh'=2,'c'=2] {'zl','zh'}, dimensions={0} | all-to-all | bytes 589824 | tf_op jit(solution)/shard_map/all_to_all | solution.py:23
  100.4 4.3 %shard_map.78 = (bf16[32,8,512]{2,1,0:T(8,128)(2,1)S(1)}, bf16[128,448]{1,0:T(8,128)(2,1)S(1)}, bf16[128,448]{1,0:T(8,128)(2,1)S(1)}) custom-call(s32[6]{0:T(128)S(1)} %copy-done.9, bf16[896,1024]{1,0:T(8,128)(2,1)S(1)} %copy-done.2, bf16[16,8,1152]{2,1,0:T(8,128)(2,1)S(1)} %all_to_all.48.z_ref), custom_call_target="tpu_custom_call" | custom-call | tf_op jit(solution)/shard_map/pallas_call | solution.py:78
  104.7 17.0 %all_to_all.49.parts_ref = bf16[32,8,512]{2,1,0:T(8,128)(2,1)S(1)} all-to-all(bf16[32,8,512]{2,1,0:T(8,128)(2,1)S(1)} %get-tuple-element.36), channel_id=1, replica_groups=mesh['y'=4,'x'=4,'zl'=8,'zh'=2,'c'=2] {'c','y','x'}, dimensions={0} | all-to-all | bytes 524288 | tf_op jit(solution)/shard_map/all_to_all | solution.py:23
  121.7 0.6 shard_map.79
  122.3 12.4 %all_to_all.50.step_ref = bf16[32,8,512]{2,1,0:T(8,128)(2,1)S(1)} all-to-all(bf16[32,8,512]{2,1,0:T(8,128)(2,1)S(1)} %shard_map.79), channel_id=1, replica_groups=mesh['y'=4,'x'=4,'zl'=8,'zh'=2,'c'=2] {'c','y','x'}, dimensions={0} | all-to-all | bytes 524288 | tf_op jit(solution)/shard_map/all_to_all | solution.py:23
  134.7 2.5 %shard_map.80 = (bf16[16,8,512]{2,1,0:T(8,128)(2,1)S(1)}, bf16[8,1024]{1,0:T(8,128)(2,1)S(1)}) custom-call(s32[6]{0:T(128)S(1)} %copy-done.9, bf16[1024,896]{1,0:T(8,128)(2,1)S(1)} %copy-done.1, bf16[32,8,512]{2,1,0:T(8,128)(2,1)S(1)} %all_to_all.50.step_ref, bf16[128,1024]{1,0:T(8,128)(2,1)S(1)} %copy-done.5, bf16[1,1024]{1,0:T(2,128)(2,1)S(1)} %copy-done.11, ...), custom_call_target="tpu_custom_call" | custom-call | tf_op jit(solution)/shard_map/pallas_call | solution.py:78
  137.1 17.7 %all_to_all.51.parts_ref = bf16[16,8,512]{2,1,0:T(8,128)(2,1)S(1)} all-to-all(bf16[16,8,512]{2,1,0:T(8,128)(2,1)S(1)} %get-tuple-element.41), channel_id=1, replica_groups=mesh['y'=4,'x'=4,'zl'=8,'zh'=2,'c'=2] {'zl','zh'}, dimensions={0} | all-to-all | bytes 262144 | tf_op jit(solution)/shard_map/all_to_all | solution.py:23
  154.8 0.6 shard_map.81
  155.5 17.6 %all_to_all.52.z_ref = bf16[16,8,512]{2,1,0:T(8,128)(2,1)S(1)} all-to-all(bf16[16,8,512]{2,1,0:T(8,128)(2,1)S(1)} %shard_map.81), channel_id=1, replica_groups=mesh['y'=4,'x'=4,'zl'=8,'zh'=2,'c'=2] {'zl','zh'}, dimensions={0} | all-to-all | bytes 262144 | tf_op jit(solution)/shard_map/all_to_all | solution.py:23
  173.1 2.1 %shard_map.82 = bf16[32,8,1024]{2,1,0:T(8,128)(2,1)S(1)} custom-call(s32[6]{0:T(128)S(1)} %copy-done.9, bf16[896,1024]{1,0:T(8,128)(2,1)S(1)} %copy-done.2, bf16[16,8,512]{2,1,0:T(8,128)(2,1)S(1)} %all_to_all.52.z_ref, bf16[128,448]{1,0:T(8,128)(2,1)S(1)} %get-tuple-element.42.pre_ref, bf16[256,512]{1,0:T(8,128)(2,1)S(1)} %get-tuple-element.31.kept_ref, ...), custom_call_target="tpu_custom_call" | custom-call | tf_op jit(solution)/shard_map/pallas_call | solution.py:78
  175.2 17.8 %all_to_all.53 = bf16[32,8,1024]{2,1,0:T(8,128)(2,1)S(1)} all-to-all(bf16[32,8,1024]{2,1,0:T(8,128)(2,1)S(1)} %shard_map.82), channel_id=1, replica_groups=mesh['y'=4,'x'=4,'zl'=8,'zh'=2,'c'=2] {'c','y','x'}, dimensions={0} | all-to-all | bytes 1048576 | tf_op jit(solution)/shard_map/all_to_all | solution.py:23
  192.9 0.1 convert_reduce_fusion
  193.0 0.6 fusion
  (19 shorter events, 0.0 us)
Async XLA Ops:
  1.3 6.9 %copy-start.10 = (bf16[1,1024]{1,0:T(2,128)(2,1)}, bf16[1,1024]{1,0:T(2,128)(2,1)S(1)}, u32[]{:S(2)}) copy-start(bf16[1,1024]{1,0:T(2,128)(2,1)S(1)} %broadcast_in_dim.6.gain_ref) | copy-start | bytes 6148
  1.4 6.2 %copy-start.8 = (s32[6]{0:T(128)}, s32[6]{0:T(128)S(1)}, u32[]{:S(2)}) copy-start(s32[6]{0:T(128)S(1)} %stack.24.place) | copy-start | bytes 76
  1.4 1.5 copy-start
  2.9 1.2 copy-start.3
  4.1 0.9 copy-start.4
  5.1 0.7 copy-start.12
  7.6 0.7 copy-start.6
  8.3 21.9 %collective-permute-start = (bf16[256,512]{1,0:T(8,128)(2,1)}, bf16[256,512]{1,0:T(8,128)(2,1)}, u32[]{:S(2)}, u32[]{:S(2)}) collective-permute-start(bf16[256,512]{1,0:T(8,128)(2,1)} %get-tuple-element.24), channel_id=1, source_target_pairs={{0,1},{1,0},{2,3},{3,2},{4,5},{5,4},{6,7},{7,6},{8,9},{9,8},{10,11... | collective-permute-start | bytes 786440 | tf_op jit(solution)/shard_map/ppermute | solution.py:373
  19.8 80.6 %copy-start.2 = (bf16[896,1024]{1,0:T(8,128)(2,1)S(1)}, bf16[896,1024]{1,0:T(8,128)(2,1)}, u32[]{:S(2)}) copy-start(bf16[896,1024]{1,0:T(8,128)(2,1)} %down_hbm.3) | copy-start | bytes 5505028
  30.2 0.6 copy-start.9
  43.0 0.9 copy-start.7
  100.4 34.3 %copy-start.1 = (bf16[1024,896]{1,0:T(8,128)(2,1)S(1)}, bf16[1024,896]{1,0:T(8,128)(2,1)}, u32[]{:S(2)}) copy-start(bf16[1024,896]{1,0:T(8,128)(2,1)} %up_hbm.3) | copy-start | bytes 5505028
  100.4 34.3 %copy-start.5 = (bf16[128,1024]{1,0:T(8,128)(2,1)S(1)}, bf16[128,1024]{1,0:T(8,128)(2,1)}, u32[]{:S(2)}) copy-start(bf16[128,1024]{1,0:T(8,128)(2,1)} %pool_ref.2) | copy-start | bytes 786436
  100.4 34.3 %copy-start.11 = (bf16[1,1024]{1,0:T(2,128)(2,1)S(1)}, bf16[1,1024]{1,0:T(2,128)(2,1)}, u32[]{:S(2)}) copy-start(bf16[1,1024]{1,0:T(2,128)(2,1)} %copy-done.10) | copy-start | bytes 6148

commit v5 on v3

--- a/solution.py
+++ b/solution.py
@@ -7,6 +7,7 @@
 from jax.experimental.pallas import tpu as pltpu
 from jax.sharding import Mesh
 from jax.sharding import PartitionSpec as P
+
 
 D = 8192
 RANK = 128
@@ -20,10 +21,6 @@
 
 def swap(x, axis):
     return lax.all_to_all(x, axis, split_axis=0, concat_axis=0, tiled=True)
-
-
-def sent_to_all(x, axis):
-    return swap(jnp.broadcast_to(x, (lax.axis_size(axis), *x.shape)), axis)
 
 
 def dot(a, b):
@@ -168,8 +165,17 @@
     up_out_ref[...] = own_half(place, dot(gained, up_ref[...])).astype(BF)
 
 
-def spread_kernel(place, parts_ref, out_ref):
-    out_ref[...] = jnp.broadcast_to(total(parts_ref).astype(BF), out_ref.shape)
+def spread_kernel(place, parts_ref, out_ref, share_ref):
+    share = total(parts_ref).astype(BF)
+    share_ref[...] = share
+    out_ref[...] = jnp.broadcast_to(share, out_ref.shape)
+
+
+def step_spread_kernel(place, parts_ref, basis_ref, out_ref):
+    rows = out_ref.shape[1]
+    basis = basis_ref[...].astype(F32)
+    share = jnp.concatenate([total(parts_ref), basis[:rows], basis[rows:]], axis=1)
+    out_ref[...] = jnp.broadcast_to(share.astype(BF), out_ref.shape)
 
 
 def moved_kernel(place, basis_ref, kept_ref, got_ref, pool_ref, up_ref, squares_ref, out_ref):
@@ -238,11 +244,13 @@
     def refine(state):
         count, _, inverse = state
         left = eye - precise(unit, inverse)
-        return count + 1, jnp.sum(left * left), inverse + precise(inverse, left)
+        moved = dot(inverse.astype(BF), left.astype(BF))
+        return count + 1, jnp.sum(left * left), inverse + moved
 
     _, _, inverse = lax.while_loop(going, refine, (0, jnp.float32(1.0), start))
-    moved = gathered[:, :half].astype(F32) * scale_col
-    coef = (precise(inverse, moved) * scale_col).astype(BF)
+    hi, lo = hi_lo(inverse * scale_col * scale_row)
+    moved = gathered[:, :half]
+    coef = (dot(hi.astype(BF), moved) + dot(lo.astype(BF), moved)).astype(BF)
     coef_ref[...] = coef
     pre = gathered[:, half : 2 * half].astype(F32) + dot(gathered[:, 2 * half + RANK :], coef)
     pre_ref[...] = pre.astype(BF)
@@ -255,23 +263,27 @@
 
 
 def second_kernel(
-    place, up_hbm, step_ref, pool_ref, gain_ref, basis_ref, coef_ref, kept_ref, got_ref, out_ref, rows_ref, up_ref, sem
+    place, step_ref, pool_ref, gain_ref, up_ref, basis_ref, coef_ref, kept_ref, got_ref, out_ref, rows_ref
 ):
     z_half = place[1]
-    count, rows, width = step_ref.shape
     pool_rows = pool_ref.shape[0]
-    start = pl.multiple_of(z_half * width, width)
-    copy = pltpu.make_async_copy(up_hbm.at[pl.ds(start, width)], up_ref, sem.at[0])
-    copy.start()
     half = coef_ref.shape[1]
-    basis = basis_ref[...].reshape(width, RANK)
-    step = step_ref[...].astype(F32).reshape(2, pool_rows, width)
+    basis = basis_ref[...].reshape(-1, RANK)
+    width = basis.shape[0]
+    wide = step_ref[...].astype(F32)
+    other = jnp.concatenate(
+        [wide[:, :, width : width + RANK], wide[:, :, width + RANK :]], axis=1
+    ).reshape(width, RANK).astype(BF)
+    step = wide[:, :, :width].reshape(2, pool_rows, width)
     pool = pool_ref[...]
     left = (pool[:, :width].astype(F32) + step[0]).astype(BF)
     right = (pool[:, width:].astype(F32) + step[1]).astype(BF)
     carried = jnp.concatenate([left, right], axis=1)
-    gain = jnp.where(z_half == 0, gain_ref[:, :width], gain_ref[:, width:])
-    gained = (jnp.where(z_half == 0, left, right).astype(F32) * gain).astype(BF)
+    gained_left = (left.astype(F32) * gain_ref[:, :width]).astype(BF)
+    gained_right = (right.astype(F32) * gain_ref[:, width:]).astype(BF)
+    gained = jnp.concatenate([gained_left, gained_right], axis=1)
+    gained_own = jnp.where(z_half == 0, gained_left, gained_right)
+    gained_other = jnp.where(z_half == 0, gained_right, gained_left)
 
     def second(one, two):
         return (dot(one, carried) + dot(two, pool)).astype(BF)
@@ -287,14 +299,12 @@
     rows_ref[...] = second(
         dot(here, chosen(tokens, 0)).astype(BF), dot(here, chosen(tokens, 1)).astype(BF)
     )
-    lane = lax.broadcasted_iota(jnp.int32, (pool_rows, out_ref.shape[2] - half), 1)
-    first = 4 * z_half
+    lane = lax.broadcasted_iota(jnp.int32, (pool_rows, RANK // 2), 1)
     tail = jnp.zeros(lane.shape, F32)
     for place_in, value in enumerate((*hi_lo(squares[:pool_rows]), *hi_lo(squares[pool_rows:]))):
-        tail = jnp.where(lane == first + place_in, value, tail)
-    low = dot(dot(gained, basis).astype(BF), coef_ref[...])
-    copy.wait()
-    up = own_half(place, dot(gained, up_ref[...])) + low
+        tail = jnp.where(lane == place_in, value, tail)
+    low = dot(gained_own, basis) + dot(gained_other, other)
+    up = own_half(place, dot(gained, up_ref[...])) + dot(low.astype(BF), coef_ref[...])
     both = jnp.concatenate([up.astype(BF), tail.astype(BF)], axis=1)
     out_ref[...] = both.reshape(out_ref.shape)
 
@@ -303,7 +313,7 @@
     share = total(parts_ref)
     lane = lax.broadcasted_iota(jnp.int32, share.shape, 1)
     out = share
-    for first in range(half, half + 8, 2):
+    for first in range(half, half + 4, 2):
         whole = jnp.where(jnp.logical_or(lane == first, lane == first + 1), share, 0.0)
         hi, lo = hi_lo(jnp.sum(whole, axis=1, keepdims=True))
         out = jnp.where(lane == first, hi, jnp.where(lane == first + 1, lo, out))
@@ -313,14 +323,13 @@
 def last_kernel(place, down_hbm, z_ref, pre_ref, kept_ref, got_ref, out_ref, down_ref, sem):
     copy = down_copy(place, down_hbm, down_ref, sem)
     copy.start()
-    z_half = place[1]
     half = pre_ref.shape[1]
     pool_rows = pre_ref.shape[0]
     gathered = z_ref[...].reshape(pool_rows, z_ref.shape[2])
     lane = lax.broadcasted_iota(jnp.int32, gathered.shape, 1)
 
     def squares(first):
-        first = half + 4 * z_half + first
+        first = half + first
         chosen = jnp.logical_or(lane == first, lane == first + 1)
         return jnp.sum(jnp.where(chosen, gathered.astype(F32), 0.0), axis=1, keepdims=True)
 
@@ -332,7 +341,7 @@
     out_ref[...] = dot(hidden, down_ref[...]).astype(BF).reshape(out_ref.shape)
 
 
-def local(weight_delta, sketch_seed, up_weight, down_weight, norm_gain, state_pool, token_rows):
+def staged(weight_delta, sketch_seed, up_weight, down_weight, norm_gain, state_pool, token_rows):
     learner = lax.axis_index(L)
     rows, cols = weight_delta.shape
     half = cols // 2
@@ -363,17 +372,20 @@
     gain = norm_gain.astype(F32)[None]
     up_scratch = (pltpu.VMEM((width, cols), BF),)
     down_scratch = (pltpu.VMEM((half, 2 * width), BF),)
+    parts, received, kept, place, gain, pool = lax.optimization_barrier(
+        (parts, received, kept, place, gain, state_pool)
+    )
+    spread, range_share = call(
+        spread_kernel, ((32, rows // 16, RANK), (rows // 16, RANK)), place, parts
+    )
+    other_share = lax.ppermute(range_share, "zh", [(0, 1), (1, 0)])
+    basis = swap(spread, CL)
     gained, pool_up, squares = call(
         pool_kernel,
         ((count, width), (count, half), (2, count, RANK)),
-        place, state_pool, gain,
+        place, pool, gain,
         hbm=up_weight, scratch=up_scratch,
     )
-    parts, received, gained, pool_up, squares, kept, place, gain, pool = lax.optimization_barrier(
-        (parts, received, gained, pool_up, squares, kept, place, gain, state_pool)
-    )
-    (spread,) = call(spread_kernel, ((32, rows // 16, RANK),), place, parts)
-    basis = swap(spread, CL)
     (stacked,) = call(
         moved_kernel,
         ((16, count // 16, 2 * half + 2 * RANK),),
@@ -386,21 +398,24 @@
         place, swap(share, Z),
         hbm=down_weight, scratch=down_scratch,
     )
-    (spread,) = call(spread_kernel, (step_part.shape,), place, swap(step_part, CL))
+    (spread,) = call(
+        step_spread_kernel,
+        ((*step_part.shape[:2], width + 2 * RANK),),
+        place, swap(step_part, CL), other_share,
+    )
     step = swap(spread, CL)
     stacked, own_second = call(
         second_kernel,
-        ((16, count // 16, padded), (out_rows, 2 * width)),
-        place, step, pool, gain, basis, coef, kept, received,
-        hbm=up_weight, scratch=up_scratch,
+        ((8, count // 8, padded), (out_rows, 2 * width)),
+        place, step, pool, gain, up_weight, basis, coef, kept, received,
     )
     (share,) = call(
-        functools.partial(second_share_kernel, half), (stacked.shape,), place, swap(stacked, Z)
+        functools.partial(second_share_kernel, half), (stacked.shape,), place, swap(stacked, "zl")
     )
     (last,) = call(
         last_kernel,
         ((32, out_rows, 2 * width),),
-        place, swap(share, Z), pool_pre, kept, received,
+        place, swap(share, "zl"), pool_pre, kept, received,
         hbm=down_weight, scratch=down_scratch,
     )
     last_share = jnp.sum(swap(last, CL).astype(F32), axis=0)
@@ -412,7 +427,7 @@
         mesh.devices.reshape(4, 4, mesh.shape["rollout"], 2, 2), ("y", "x", "zl", "zh", "c")
     )
     return jax.shard_map(
-        local,
+        staged,
         mesh=torus,
         in_specs=(
             P(("zl", "zh", "c"), L),

time: 187 us -> 193 us (1.032)
  blocking collectives: 149 us -> 120 us
  starting transfers between devices: 12.2 us -> 29.4 us
  waiting for transfers between devices: 2.28 us -> 19.3 us
    all_to_all x8 -> x6, blocking collectives: 149 us -> 120 us  [swap(): return lax.all_to_all(x, axis, split_axis=0, concat_axis=0, tiled=True)]
    all_to_all x1 -> x3, starting transfers between devices: 3.5 us -> 17 us  [swap(): return lax.all_to_all(x, axis, split_axis=0, concat_axis=0, tiled=True)]
    ppermute x1 -> x2, waiting for transfers between devices: 0.01 us -> 9.42 us  [the longest x1 9.42 us: staged(): other_share = lax.ppermute(range_share, 'zh', [(0, 1), (1, 0)])]
    all_to_all x1 -> x3, waiting for transfers between devices: 2.28 us -> 9.83 us  [swap(): return lax.all_to_all(x, axis, split_axis=0, concat_axis=0, tiled=True)]
    ppermute x1 -> x2, starting transfers between devices: 8.75 us -> 12.4 us  [the longest x1 8.75 us: staged(): received = lax.ppermute(sent, 'c', [(0, 1), (1, 0)])]
    unnamed x14 -> x16, local copies, waits for them, and re-layouts: 4.32 us -> 4.32 us
  transfers between devices with their start and end apart: 2 -> 5, of which waited for: 1 -> 3; matrix products, arithmetic and copies ran while one was open for 0% -> 0% of each run, Pallas kernels for 1% -> 1%
where the time goes in v5:
time: 193 us; the launch traced here: 192 us
  blocking collectives  120 us (62%)
  starting transfers between devices  29.4 us (15%)
  waiting for transfers between devices  19.3 us (10%)
  Pallas kernels  16.3 us (8%)
  local copies, waits for them, and re-layouts  4.4 us (2%)
    all_to_all x6, blocking collectives, swap(): return lax.all_to_all(x, axis, split_axis=0, concat_axis=0, tiled=True)  120 us
    all_to_all x3, starting transfers between devices, swap(): return lax.all_to_all(x, axis, split_axis=0, concat_axis=0, tiled=True)  17 us
    pallas_call x10, Pallas kernels, call(): pl.pallas_call(kernel, out_shape=tuple((jax.ShapeDtypeStruct(shape, BF) f...  16.3 us
    all_to_all x3, waiting for transfers between devices, swap(): return lax.all_to_all(x, axis, split_axis=0, concat_axis=0, tiled=True)  9.83 us
    ppermute x1, waiting for transfers between devices, staged(): other_share = lax.ppermute(range_share, 'zh', [(0, 1), (1, 0)])  9.42 us
    ppermute x1, starting transfers between devices, staged(): received = lax.ppermute(sent, 'c', [(0, 1), (1, 0)])  8.75 us
    unnamed x16, local copies, waits for them, and re-layouts  4.32 us
  transfers between devices with their start and end apart: 5, of which 3 were waited for; matrix products, arithmetic and copies ran while one was open for 0% of the time, Pallas kernels for 1%

profile of v5, /device:TPU:1, one launch (start us, length us, event | category | flops | bytes accessed | tf_op | source)
XLA Modules:
  0.0 191.8 jit_solution(12564150410915830529)
XLA Ops:
  0.7 0.1 stack.24.place
  0.7 1.2 copy-done.6
  1.9 0.7 copy-done.7
  2.6 2.6 %shard_map.73 = (bf16[16,16,128]{2,1,0:T(8,128)(2,1)}, bf16[256,512]{1,0:T(8,128)(2,1)S(1)}, bf16[256,512]{1,0:T(8,128)(2,1)S(1)}) custom-call(s32[6]{0:T(128)S(1)} %stack.24.place, f32[256,896]{1,0:T(8,128)S(1)} %copy-done.6, s32[2,128]{1,0:T(2,128)S(1)} %bitcast.11), custom_call_target="tpu_custom_call" | custom-call | tf_op jit(solution)/shard_map/pallas_call | solution.py:78
  5.2 8.7 %collective-permute-start = (bf16[256,512]{1,0:T(8,128)(2,1)S(1)}, bf16[256,512]{1,0:T(8,128)(2,1)S(1)}, u32[]{:S(2)}, u32[]{:S(2)}) collective-permute-start(bf16[256,512]{1,0:T(8,128)(2,1)S(1)} %get-tuple-element.25), channel_id=1, source_target_pairs={{0,1},{1,0},{2,3},{3,2},{4,5},{5,4},{6,7},{7,6},{8,9},{9,8},{10,11... | collective-permute-start | bytes 786440 | tf_op jit(solution)/shard_map/ppermute | solution.py:370
  14.0 3.5 %all-to-all-start = ((bf16[16,16,128]{2,1,0:T(8,128)(2,1)}), bf16[16,16,128]{2,1,0:T(8,128)(2,1)S(1)}, u32[]{:S(2)}, u32[]{:S(2)}) async-start(bf16[16,16,128]{2,1,0:T(8,128)(2,1)} %get-tuple-element.24), calls=%async_computation | async-start | bytes 131072 | tf_op jit(solution)/shard_map/all_to_all | solution.py:23
  17.5 0.7 broadcast_in_dim.12
  18.1 6.1 %all-to-all-done.parts_ref = bf16[16,16,128]{2,1,0:T(8,128)(2,1)S(1)} async-done(((bf16[16,16,128]{2,1,0:T(8,128)(2,1)}), bf16[16,16,128]{2,1,0:T(8,128)(2,1)S(1)}, u32[]{:S(2)}, u32[]{:S(2)}) %all-to-all-start) | async-done | bytes 65568 | tf_op jit(solution)/shard_map/all_to_all | solution.py:23
  24.2 1.2 shard_map.74
  25.5 4.5 %all-to-all-start.1 = ((bf16[32,16,128]{2,1,0:T(8,128)(2,1)}), bf16[32,16,128]{2,1,0:T(8,128)(2,1)S(1)}, u32[]{:S(2)}, u32[]{:S(2)}) async-start(bf16[32,16,128]{2,1,0:T(8,128)(2,1)} %get-tuple-element.29), calls=%async_computation.1 | async-start | bytes 262144 | tf_op jit(solution)/shard_map/all_to_all | solution.py:23
  29.9 1.5 copy-done
  31.4 0.9 copy-done.4
  32.4 1.3 shard_map.75
  33.7 3.8 %all-to-all-done.1.basis_ref = bf16[32,16,128]{2,1,0:T(8,128)(2,1)S(1)} async-done(((bf16[32,16,128]{2,1,0:T(8,128)(2,1)}), bf16[32,16,128]{2,1,0:T(8,128)(2,1)S(1)}, u32[]{:S(2)}, u32[]{:S(2)}) %all-to-all-start.1) | async-done | bytes 131104 | tf_op jit(solution)/shard_map/all_to_all | solution.py:23
  37.5 0.9 shard_map.76
  38.4 30.7 %all_to_all.45.parts_ref = bf16[16,8,1152]{2,1,0:T(8,128)(2,1)S(1)} all-to-all(bf16[16,8,1152]{2,1,0:T(8,128)(2,1)S(1)} %shard_map.76), channel_id=1, replica_groups=mesh['y'=4,'x'=4,'zl'=8,'zh'=2,'c'=2] {'zl','zh'}, dimensions={0} | all-to-all | bytes 589824 | tf_op jit(solution)/shard_map/all_to_all | solution.py:23
  69.1 0.7 shard_map.77
  69.8 23.8 %all_to_all.46.z_ref = bf16[16,8,1152]{2,1,0:T(8,128)(2,1)S(1)} all-to-all(bf16[16,8,1152]{2,1,0:T(8,128)(2,1)S(1)} %shard_map.77), channel_id=1, replica_groups=mesh['y'=4,'x'=4,'zl'=8,'zh'=2,'c'=2] {'zl','zh'}, dimensions={0} | all-to-all | bytes 589824 | tf_op jit(solution)/shard_map/all_to_all | solution.py:23
  93.5 5.0 %shard_map.78 = (bf16[32,8,512]{2,1,0:T(8,128)(2,1)}, bf16[128,448]{1,0:T(8,128)(2,1)S(1)}, bf16[128,448]{1,0:T(8,128)(2,1)S(1)}) custom-call(s32[6]{0:T(128)S(1)} %stack.24.place, bf16[896,1024]{1,0:T(8,128)(2,1)S(1)} %copy-done.2, bf16[16,8,1152]{2,1,0:T(8,128)(2,1)S(1)} %all_to_all.46.z_ref), custom_call_target="tpu_custom_call" | custom-call | tf_op jit(solution)/shard_map/pallas_call | solution.py:78
  98.6 9.0 %all-to-all-start.4 = ((bf16[32,8,512]{2,1,0:T(8,128)(2,1)}), bf16[32,8,512]{2,1,0:T(8,128)(2,1)S(1)}, u32[]{:S(2)}, u32[]{:S(2)}) async-start(bf16[32,8,512]{2,1,0:T(8,128)(2,1)} %get-tuple-element.37), calls=%async_computation.4 | async-start | bytes 524288 | tf_op jit(solution)/shard_map/all_to_all | solution.py:23
  107.6 3.6 %collective-permute-start.1 = (bf16[16,128]{1,0:T(8,128)(2,1)S(1)}, bf16[16,128]{1,0:T(8,128)(2,1)S(1)}, u32[]{:S(2)}, u32[]{:S(2)}) collective-permute-start(bf16[16,128]{1,0:T(8,128)(2,1)S(1)} %get-tuple-element.38), channel_id=1, source_target_pairs={{0,2},{2,0},{1,3},{3,1},{4,6},{6,4},{5,7},{7,5},{8,10},{10,8},{9,1... | collective-permute-start | bytes 12296 | tf_op jit(solution)/shard_map/ppermute | solution.py:381
  111.2 9.4 %collective-permute-done.1.basis_ref = bf16[16,128]{1,0:T(8,128)(2,1)S(1)} collective-permute-done((bf16[16,128]{1,0:T(8,128)(2,1)S(1)}, bf16[16,128]{1,0:T(8,128)(2,1)S(1)}, u32[]{:S(2)}, u32[]{:S(2)}) %collective-permute-start.1) | collective-permute-done | bytes 4128 | tf_op jit(solution)/shard_map/ppermute | solution.py:381
  120.6 0.6 shard_map.79
  121.2 17.7 %all_to_all.47.step_ref = bf16[32,8,768]{2,1,0:T(8,128)(2,1)S(1)} all-to-all(bf16[32,8,768]{2,1,0:T(8,128)(2,1)S(1)} %shard_map.79), channel_id=1, replica_groups=mesh['y'=4,'x'=4,'zl'=8,'zh'=2,'c'=2] {'c','y','x'}, dimensions={0} | all-to-all | bytes 786432 | tf_op jit(solution)/shard_map/all_to_all | solution.py:23
  139.0 1.7 shard_map.80
  140.7 14.2 %all_to_all.48.parts_ref = bf16[8,16,512]{2,1,0:T(8,128)(2,1)S(1)} all-to-all(bf16[8,16,512]{2,1,0:T(8,128)(2,1)S(1)} %get-tuple-element.41), channel_id=1, replica_groups=mesh['y'=4,'x'=4,'zl'=8,'zh'=2,'c'=2] {'zl'}, dimensions={0} | all-to-all | bytes 262144 | tf_op jit(solution)/shard_map/all_to_all | solution.py:23
  154.9 0.6 shard_map.81
  155.5 15.4 %all_to_all.49.z_ref = bf16[8,16,512]{2,1,0:T(8,128)(2,1)S(1)} all-to-all(bf16[8,16,512]{2,1,0:T(8,128)(2,1)S(1)} %shard_map.81), channel_id=1, replica_groups=mesh['y'=4,'x'=4,'zl'=8,'zh'=2,'c'=2] {'zl'}, dimensions={0} | all-to-all | bytes 262144 | tf_op jit(solution)/shard_map/all_to_all | solution.py:23
  170.9 1.7 shard_map.82
  172.6 18.5 %all_to_all.50 = bf16[32,8,1024]{2,1,0:T(8,128)(2,1)S(1)} all-to-all(bf16[32,8,1024]{2,1,0:T(8,128)(2,1)S(1)} %shard_map.82), channel_id=1, replica_groups=mesh['y'=4,'x'=4,'zl'=8,'zh'=2,'c'=2] {'c','y','x'}, dimensions={0} | all-to-all | bytes 1048576 | tf_op jit(solution)/shard_map/all_to_all | solution.py:23
  191.1 0.1 convert_reduce_fusion
  191.2 0.6 fusion
  (14 shorter events, 0.0 us)
Async XLA Ops:
  0.7 1.2 copy-start.6
  1.9 0.7 copy-start.7
  5.2 19.0 %collective-permute-start = (bf16[256,512]{1,0:T(8,128)(2,1)S(1)}, bf16[256,512]{1,0:T(8,128)(2,1)S(1)}, u32[]{:S(2)}, u32[]{:S(2)}) collective-permute-start(bf16[256,512]{1,0:T(8,128)(2,1)S(1)} %get-tuple-element.25), channel_id=1, source_target_pairs={{0,1},{1,0},{2,3},{3,2},{4,5},{5,4},{6,7},{7,6},{8,9},{9,8},{10,11... | collective-permute-start | bytes 786440 | tf_op jit(solution)/shard_map/ppermute | solution.py:370
  14.0 10.3 %all-to-all-start = ((bf16[16,16,128]{2,1,0:T(8,128)(2,1)}), bf16[16,16,128]{2,1,0:T(8,128)(2,1)S(1)}, u32[]{:S(2)}, u32[]{:S(2)}) async-start(bf16[16,16,128]{2,1,0:T(8,128)(2,1)} %get-tuple-element.24), calls=%async_computation | async-start | bytes 131072 | tf_op jit(solution)/shard_map/all_to_all | solution.py:23
  25.5 12.0 %all-to-all-start.1 = ((bf16[32,16,128]{2,1,0:T(8,128)(2,1)}), bf16[32,16,128]{2,1,0:T(8,128)(2,1)S(1)}, u32[]{:S(2)}, u32[]{:S(2)}) async-start(bf16[32,16,128]{2,1,0:T(8,128)(2,1)} %get-tuple-element.29), calls=%async_computation.1 | async-start | bytes 262144 | tf_op jit(solution)/shard_map/all_to_all | solution.py:23
  29.9 1.5 copy-start
  31.4 0.9 copy-start.4
  37.5 56.1 %copy-start.2 = (bf16[896,1024]{1,0:T(8,128)(2,1)S(1)}, bf16[896,1024]{1,0:T(8,128)(2,1)}, u32[]{:S(2)}) copy-start(bf16[896,1024]{1,0:T(8,128)(2,1)} %down_hbm.3) | copy-start | bytes 5505028
  93.5 45.5 %copy-start.1 = (bf16[1024,896]{1,0:T(8,128)(2,1)S(1)}, bf16[1024,896]{1,0:T(8,128)(2,1)}, u32[]{:S(2)}) copy-start(bf16[1024,896]{1,0:T(8,128)(2,1)} %up_ref.1) | copy-start | bytes 5505028
  93.5 45.5 %copy-start.5 = (bf16[128,1024]{1,0:T(8,128)(2,1)S(1)}, bf16[128,1024]{1,0:T(8,128)(2,1)}, u32[]{:S(2)}) copy-start(bf16[128,1024]{1,0:T(8,128)(2,1)} %pool_ref.1) | copy-start | bytes 786436
  98.6 22.1 %all-to-all-start.4 = ((bf16[32,8,512]{2,1,0:T(8,128)(2,1)}), bf16[32,8,512]{2,1,0:T(8,128)(2,1)S(1)}, u32[]{:S(2)}, u32[]{:S(2)}) async-start(bf16[32,8,512]{2,1,0:T(8,128)(2,1)} %get-tuple-element.37), calls=%async_computation.4 | async-start | bytes 524288 | tf_op jit(solution)/shard_map/all_to_all | solution.py:23
  107.6 13.1 %collective-permute-start.1 = (bf16[16,128]{1,0:T(8,128)(2,1)S(1)}, bf16[16,128]{1,0:T(8,128)(2,1)S(1)}, u32[]{:S(2)}, u32[]{:S(2)}) collective-permute-start(bf16[16,128]{1,0:T(8,128)(2,1)S(1)} %get-tuple-element.38), channel_id=1, source_target_pairs={{0,2},{2,0},{1,3},{3,1},{4,6},{6,4},{5,7},{7,5},{8,10},{10,8},{9,1... | collective-permute-start | bytes 12296 | tf_op jit(solution)/shard_map/ppermute | solution.py:381
  139.0 32.0 %copy-start.3 = (bf16[896,1024]{1,0:T(8,128)(2,1)S(1)}, bf16[896,1024]{1,0:T(8,128)(2,1)}, u32[]{:S(2)}) copy-start(bf16[896,1024]{1,0:T(8,128)(2,1)} %down_hbm.3) | copy-start | bytes 5505028

commit v6 on v5

--- a/solution.py
+++ b/solution.py
@@ -147,6 +147,11 @@
         sent_ref[span] = jnp.concatenate([jnp.where(core == 0, right, left), tokens], axis=1)
 
 
+def pick_kernel(place, kept_ref, got_ref, pick_ref):
+    for step in range(2):
+        pick_ref[step] = picks(place, kept_ref, got_ref, step)
+
+
 def pool_kernel(place, up_hbm, pool_ref, gain_ref, gained_ref, up_out_ref, squares_ref, up_ref, sem):
     z_half = place[1]
     width = up_ref.shape[0]
@@ -263,11 +268,10 @@
 
 
 def second_kernel(
-    place, step_ref, pool_ref, gain_ref, up_ref, basis_ref, coef_ref, kept_ref, got_ref, out_ref, rows_ref
+    place, step_ref, pool_ref, gain_ref, up_ref, basis_ref, coef_ref, pick_ref, out_ref, rows_ref
 ):
     z_half = place[1]
     pool_rows = pool_ref.shape[0]
-    half = coef_ref.shape[1]
     basis = basis_ref[...].reshape(-1, RANK)
     width = basis.shape[0]
     wide = step_ref[...].astype(F32)
@@ -288,17 +292,16 @@
     def second(one, two):
         return (dot(one, carried) + dot(two, pool)).astype(BF)
 
-    wide = second(
-        picks(place, kept_ref, got_ref, 0), picks(place, kept_ref, got_ref, 1)
-    ).astype(F32)
+    wide = second(pick_ref[0], pick_ref[1]).astype(F32)
     squares = jnp.sum(wide * wide, axis=1, keepdims=True)
     row = lax.broadcasted_iota(jnp.int32, (rows_ref.shape[0], pool_rows), 0)
     lane = lax.broadcasted_iota(jnp.int32, (rows_ref.shape[0], pool_rows), 1)
     here = jnp.where(lane == row + place[5], 1.0, 0.0).astype(BF)
-    tokens = kept_ref[:, half : half + 1]
-    rows_ref[...] = second(
-        dot(here, chosen(tokens, 0)).astype(BF), dot(here, chosen(tokens, 1)).astype(BF)
-    )
+    own = [
+        dot(here, jnp.where(place[0] == 0, pick_ref[i, :pool_rows], pick_ref[i, pool_rows:]))
+        for i in range(2)
+    ]
+    rows_ref[...] = second(own[0].astype(BF), own[1].astype(BF))
     lane = lax.broadcasted_iota(jnp.int32, (pool_rows, RANK // 2), 1)
     tail = jnp.zeros(lane.shape, F32)
     for place_in, value in enumerate((*hi_lo(squares[:pool_rows]), *hi_lo(squares[pool_rows:]))):
@@ -320,7 +323,7 @@
     out_ref[...] = jnp.broadcast_to(out.astype(BF), out_ref.shape)
 
 
-def last_kernel(place, down_hbm, z_ref, pre_ref, kept_ref, got_ref, out_ref, down_ref, sem):
+def last_kernel(place, down_hbm, z_ref, pre_ref, pick_ref, out_ref, down_ref, sem):
     copy = down_copy(place, down_hbm, down_ref, sem)
     copy.start()
     half = pre_ref.shape[1]
@@ -334,8 +337,7 @@
         return jnp.sum(jnp.where(chosen, gathered.astype(F32), 0.0), axis=1, keepdims=True)
 
     scale = lax.rsqrt(jnp.concatenate([squares(0), squares(2)], axis=0) / D + EPS)
-    one, two = picks(place, kept_ref, got_ref, 0), picks(place, kept_ref, got_ref, 1)
-    pre = dot(one, gathered[:, :half]) + dot(two, pre_ref[...])
+    pre = dot(pick_ref[0], gathered[:, :half]) + dot(pick_ref[1], pre_ref[...])
     hidden = silu(pre * scale).astype(BF)
     copy.wait()
     out_ref[...] = dot(hidden, down_ref[...]).astype(BF).reshape(out_ref.shape)
@@ -372,30 +374,32 @@
     gain = norm_gain.astype(F32)[None]
     up_scratch = (pltpu.VMEM((width, cols), BF),)
     down_scratch = (pltpu.VMEM((half, 2 * width), BF),)
-    parts, received, kept, place, gain, pool = lax.optimization_barrier(
-        (parts, received, kept, place, gain, state_pool)
-    )
-    spread, range_share = call(
-        spread_kernel, ((32, rows // 16, RANK), (rows // 16, RANK)), place, parts
-    )
-    other_share = lax.ppermute(range_share, "zh", [(0, 1), (1, 0)])
-    basis = swap(spread, CL)
     gained, pool_up, squares = call(
         pool_kernel,
         ((count, width), (count, half), (2, count, RANK)),
-        place, pool, gain,
+        place, state_pool, gain,
         hbm=up_weight, scratch=up_scratch,
     )
+    parts, received, gained, pool_up, squares, kept, place, gain, pool = lax.optimization_barrier(
+        (parts, received, gained, pool_up, squares, kept, place, gain, state_pool)
+    )
+    spread, range_share = call(
+        spread_kernel, ((32, rows // 16, RANK), (rows // 16, RANK)), place, parts
+    )
+    other_share = lax.ppermute(range_share, "zh", [(0, 1), (1, 0)])
+    basis = swap(spread, CL)
+    (pick,) = call(pick_kernel, ((2, 2 * count, count),), place, kept, received)
     (stacked,) = call(
         moved_kernel,
         ((16, count // 16, 2 * half + 2 * RANK),),
         place, basis, kept, received, gained, pool_up, squares,
     )
     (share,) = call(share_kernel, (stacked.shape,), place, swap(stacked, Z))
+    gathered = swap(share, Z)
     step_part, coef, pool_pre = call(
         first_kernel,
         ((32, count // 16, width), (RANK, half), (count, half)),
-        place, swap(share, Z),
+        place, gathered,
         hbm=down_weight, scratch=down_scratch,
     )
     (spread,) = call(
@@ -407,7 +411,7 @@
     stacked, own_second = call(
         second_kernel,
         ((8, count // 8, padded), (out_rows, 2 * width)),
-        place, step, pool, gain, up_weight, basis, coef, kept, received,
+        place, step, pool, gain, up_weight, basis, coef, pick,
     )
     (share,) = call(
         functools.partial(second_share_kernel, half), (stacked.shape,), place, swap(stacked, "zl")
@@ -415,7 +419,7 @@
     (last,) = call(
         last_kernel,
         ((32, out_rows, 2 * width),),
-        place, swap(share, "zl"), pool_pre, kept, received,
+        place, swap(share, "zl"), pool_pre, pick,
         hbm=down_weight, scratch=down_scratch,
     )
     last_share = jnp.sum(swap(last, CL).astype(F32), axis=0)

time: 193 us -> 193 us (level)
  blocking collectives: 120 us -> 115 us
  starting transfers between devices: 29.4 us -> 33.5 us
    all_to_all x6, blocking collectives: 120 us -> 115 us  [swap(): return lax.all_to_all(x, axis, split_axis=0, concat_axis=0, tiled=True)]
    all_to_all x3, starting transfers between devices: 17 us -> 21.1 us  [swap(): return lax.all_to_all(x, axis, split_axis=0, concat_axis=0, tiled=True)]
    pallas_call x10 -> x11, Pallas kernels: 16.3 us -> 16.9 us  [call(): pl.pallas_call(kernel, out_shape=tuple((jax.ShapeDtypeStruct(shape, BF) f...]
where the time goes in v6:
time: 193 us; the launch traced here: 192 us
  blocking collectives  115 us (60%)
  starting transfers between devices  33.5 us (17%)
  waiting for transfers between devices  20.5 us (11%)
  Pallas kernels  16.9 us (9%)
  local copies, waits for them, and re-layouts  4.41 us (2%)
    all_to_all x6, blocking collectives, swap(): return lax.all_to_all(x, axis, split_axis=0, concat_axis=0, tiled=True)  115 us
    all_to_all x3, starting transfers between devices, swap(): return lax.all_to_all(x, axis, split_axis=0, concat_axis=0, tiled=True)  21.1 us
    pallas_call x11, Pallas kernels, call(): pl.pallas_call(kernel, out_shape=tuple((jax.ShapeDtypeStruct(shape, BF) f...  16.9 us
    all_to_all x3, waiting for transfers between devices, swap(): return lax.all_to_all(x, axis, split_axis=0, concat_axis=0, tiled=True)  11.1 us
    ppermute x1, waiting for transfers between devices, staged(): other_share = lax.ppermute(range_share, 'zh', [(0, 1), (1, 0)])  9.42 us
    ppermute x1, starting transfers between devices, staged(): received = lax.ppermute(sent, 'c', [(0, 1), (1, 0)])  8.75 us
    unnamed x16, local copies, waits for them, and re-layouts  4.33 us
  transfers between devices with their start and end apart: 5, of which 3 were waited for; matrix products, arithmetic and copies ran while one was open for 0% of the time, Pallas kernels for 1%

profile of v6, /device:TPU:1, one launch (start us, length us, event | category | flops | bytes accessed | tf_op | source)
XLA Modules:
  0.0 192.3 jit_solution(11166200463970360467)
XLA Ops:
  0.7 0.1 stack.24.place
  0.7 1.2 copy-done.6
  1.9 0.7 copy-done.7
  2.6 2.6 %shard_map.73 = (bf16[16,16,128]{2,1,0:T(8,128)(2,1)}, bf16[256,512]{1,0:T(8,128)(2,1)S(1)}, bf16[256,512]{1,0:T(8,128)(2,1)S(1)}) custom-call(s32[6]{0:T(128)S(1)} %stack.24.place, f32[256,896]{1,0:T(8,128)S(1)} %copy-done.6, s32[2,128]{1,0:T(2,128)S(1)} %bitcast.11), custom_call_target="tpu_custom_call" | custom-call | tf_op jit(solution)/shard_map/pallas_call | solution.py:78
  5.2 8.7 %collective-permute-start = (bf16[256,512]{1,0:T(8,128)(2,1)S(1)}, bf16[256,512]{1,0:T(8,128)(2,1)S(1)}, u32[]{:S(2)}, u32[]{:S(2)}) collective-permute-start(bf16[256,512]{1,0:T(8,128)(2,1)S(1)} %get-tuple-element.28), channel_id=1, source_target_pairs={{0,1},{1,0},{2,3},{3,2},{4,5},{5,4},{6,7},{7,6},{8,9},{9,8},{10,11... | collective-permute-start | bytes 786440 | tf_op jit(solution)/shard_map/ppermute | solution.py:372
  14.0 3.5 %all-to-all-start = ((bf16[16,16,128]{2,1,0:T(8,128)(2,1)}), bf16[16,16,128]{2,1,0:T(8,128)(2,1)S(1)}, u32[]{:S(2)}, u32[]{:S(2)}) async-start(bf16[16,16,128]{2,1,0:T(8,128)(2,1)} %get-tuple-element.27), calls=%async_computation | async-start | bytes 131072 | tf_op jit(solution)/shard_map/all_to_all | solution.py:23
  17.5 0.7 broadcast_in_dim.11
  18.2 1.5 copy-done
  19.7 0.9 copy-done.4
  20.6 1.3 shard_map.74
  21.9 2.3 %all-to-all-done.parts_ref = bf16[16,16,128]{2,1,0:T(8,128)(2,1)S(1)} async-done(((bf16[16,16,128]{2,1,0:T(8,128)(2,1)}), bf16[16,16,128]{2,1,0:T(8,128)(2,1)S(1)}, u32[]{:S(2)}, u32[]{:S(2)}) %all-to-all-start) | async-done | bytes 65568 | tf_op jit(solution)/shard_map/all_to_all | solution.py:23
  24.2 0.6 shard_map.75
  24.8 12.3 %all_to_all.45.basis_ref = bf16[32,16,128]{2,1,0:T(8,128)(2,1)S(1)} all-to-all(bf16[32,16,128]{2,1,0:T(8,128)(2,1)S(1)} %get-tuple-element.35), channel_id=1, replica_groups=mesh['y'=4,'x'=4,'zl'=8,'zh'=2,'c'=2] {'c','y','x'}, dimensions={0} | all-to-all | bytes 262144 | tf_op jit(solution)/shard_map/all_to_all | solution.py:23
  37.1 0.9 shard_map.76
  38.0 30.8 %all_to_all.46.parts_ref = bf16[16,8,1152]{2,1,0:T(8,128)(2,1)S(1)} all-to-all(bf16[16,8,1152]{2,1,0:T(8,128)(2,1)S(1)} %shard_map.76), channel_id=1, replica_groups=mesh['y'=4,'x'=4,'zl'=8,'zh'=2,'c'=2] {'zl','zh'}, dimensions={0} | all-to-all | bytes 589824 | tf_op jit(solution)/shard_map/all_to_all | solution.py:23
  68.8 0.7 shard_map.77
  69.4 23.7 %all_to_all.47.z_ref = bf16[16,8,1152]{2,1,0:T(8,128)(2,1)S(1)} all-to-all(bf16[16,8,1152]{2,1,0:T(8,128)(2,1)S(1)} %shard_map.77), channel_id=1, replica_groups=mesh['y'=4,'x'=4,'zl'=8,'zh'=2,'c'=2] {'zl','zh'}, dimensions={0} | all-to-all | bytes 589824 | tf_op jit(solution)/shard_map/all_to_all | solution.py:23
  93.1 5.0 %shard_map.78 = (bf16[32,8,512]{2,1,0:T(8,128)(2,1)}, bf16[128,448]{1,0:T(8,128)(2,1)S(1)}, bf16[128,448]{1,0:T(8,128)(2,1)S(1)}) custom-call(s32[6]{0:T(128)S(1)} %stack.24.place, bf16[896,1024]{1,0:T(8,128)(2,1)S(1)} %copy-done.2, bf16[16,8,1152]{2,1,0:T(8,128)(2,1)S(1)} %all_to_all.47.z_ref), custom_call_target="tpu_custom_call" | custom-call | tf_op jit(solution)/shard_map/pallas_call | solution.py:78
  98.2 9.1 %all-to-all-start.4 = ((bf16[32,8,512]{2,1,0:T(8,128)(2,1)}), bf16[32,8,512]{2,1,0:T(8,128)(2,1)S(1)}, u32[]{:S(2)}, u32[]{:S(2)}) async-start(bf16[32,8,512]{2,1,0:T(8,128)(2,1)} %get-tuple-element.41), calls=%async_computation.4 | async-start | bytes 524288 | tf_op jit(solution)/shard_map/all_to_all | solution.py:23
  107.3 3.6 %collective-permute-start.1 = (bf16[16,128]{1,0:T(8,128)(2,1)S(1)}, bf16[16,128]{1,0:T(8,128)(2,1)S(1)}, u32[]{:S(2)}, u32[]{:S(2)}) collective-permute-start(bf16[16,128]{1,0:T(8,128)(2,1)S(1)} %get-tuple-element.42), channel_id=1, source_target_pairs={{0,2},{2,0},{1,3},{3,1},{4,6},{6,4},{5,7},{7,5},{8,10},{10,8},{9,1... | collective-permute-start | bytes 12296 | tf_op jit(solution)/shard_map/ppermute | solution.py:389
  111.0 9.4 %collective-permute-done.1.basis_ref = bf16[16,128]{1,0:T(8,128)(2,1)S(1)} collective-permute-done((bf16[16,128]{1,0:T(8,128)(2,1)S(1)}, bf16[16,128]{1,0:T(8,128)(2,1)S(1)}, u32[]{:S(2)}, u32[]{:S(2)}) %collective-permute-start.1) | collective-permute-done | bytes 4128 | tf_op jit(solution)/shard_map/ppermute | solution.py:389
  120.4 1.3 shard_map.79
  121.7 8.5 %all-to-all-start.5 = ((bf16[32,8,768]{2,1,0:T(8,128)(2,1)}), bf16[32,8,768]{2,1,0:T(8,128)(2,1)S(1)}, u32[]{:S(2)}, u32[]{:S(2)}) async-start(bf16[32,8,768]{2,1,0:T(8,128)(2,1)} %shard_map.79), calls=%async_computation.5 | async-start | bytes 786432 | tf_op jit(solution)/shard_map/all_to_all | solution.py:23
  130.2 0.7 shard_map.80.pick_ref
  130.9 8.8 %all-to-all-done.5.step_ref = bf16[32,8,768]{2,1,0:T(8,128)(2,1)S(1)} async-done(((bf16[32,8,768]{2,1,0:T(8,128)(2,1)}), bf16[32,8,768]{2,1,0:T(8,128)(2,1)S(1)}, u32[]{:S(2)}, u32[]{:S(2)}) %all-to-all-start.5) | async-done | bytes 393248 | tf_op jit(solution)/shard_map/all_to_all | solution.py:23
  139.7 1.6 shard_map.81
  141.3 14.2 %all_to_all.48.parts_ref = bf16[8,16,512]{2,1,0:T(8,128)(2,1)S(1)} all-to-all(bf16[8,16,512]{2,1,0:T(8,128)(2,1)S(1)} %get-tuple-element.47), channel_id=1, replica_groups=mesh['y'=4,'x'=4,'zl'=8,'zh'=2,'c'=2] {'zl'}, dimensions={0} | all-to-all | bytes 262144 | tf_op jit(solution)/shard_map/all_to_all | solution.py:23
  155.5 0.6 shard_map.82
  156.2 15.4 %all_to_all.49.z_ref = bf16[8,16,512]{2,1,0:T(8,128)(2,1)S(1)} all-to-all(bf16[8,16,512]{2,1,0:T(8,128)(2,1)S(1)} %shard_map.82), channel_id=1, replica_groups=mesh['y'=4,'x'=4,'zl'=8,'zh'=2,'c'=2] {'zl'}, dimensions={0} | all-to-all | bytes 262144 | tf_op jit(solution)/shard_map/all_to_all | solution.py:23
  171.6 1.6 shard_map.83
  173.2 18.5 %all_to_all.50 = bf16[32,8,1024]{2,1,0:T(8,128)(2,1)S(1)} all-to-all(bf16[32,8,1024]{2,1,0:T(8,128)(2,1)S(1)} %shard_map.83), channel_id=1, replica_groups=mesh['y'=4,'x'=4,'zl'=8,'zh'=2,'c'=2] {'c','y','x'}, dimensions={0} | all-to-all | bytes 1048576 | tf_op jit(solution)/shard_map/all_to_all | solution.py:23
  191.7 0.6 fusion
  (15 shorter events, 0.1 us)
Async XLA Ops:
  0.7 1.2 copy-start.6
  1.9 0.7 copy-start.7
  5.2 19.0 %collective-permute-start = (bf16[256,512]{1,0:T(8,128)(2,1)S(1)}, bf16[256,512]{1,0:T(8,128)(2,1)S(1)}, u32[]{:S(2)}, u32[]{:S(2)}) collective-permute-start(bf16[256,512]{1,0:T(8,128)(2,1)S(1)} %get-tuple-element.28), channel_id=1, source_target_pairs={{0,1},{1,0},{2,3},{3,2},{4,5},{5,4},{6,7},{7,6},{8,9},{9,8},{10,11... | collective-permute-start | bytes 786440 | tf_op jit(solution)/shard_map/ppermute | solution.py:372
  14.0 10.3 %all-to-all-start = ((bf16[16,16,128]{2,1,0:T(8,128)(2,1)}), bf16[16,16,128]{2,1,0:T(8,128)(2,1)S(1)}, u32[]{:S(2)}, u32[]{:S(2)}) async-start(bf16[16,16,128]{2,1,0:T(8,128)(2,1)} %get-tuple-element.27), calls=%async_computation | async-start | bytes 131072 | tf_op jit(solution)/shard_map/all_to_all | solution.py:23
  18.1 1.5 copy-start
  19.6 0.9 copy-start.4
  21.9 71.2 %copy-start.2 = (bf16[896,1024]{1,0:T(8,128)(2,1)S(1)}, bf16[896,1024]{1,0:T(8,128)(2,1)}, u32[]{:S(2)}) copy-start(bf16[896,1024]{1,0:T(8,128)(2,1)} %down_hbm.3) | copy-start | bytes 5505028
  98.2 41.5 %copy-start.1 = (bf16[1024,896]{1,0:T(8,128)(2,1)S(1)}, bf16[1024,896]{1,0:T(8,128)(2,1)}, u32[]{:S(2)}) copy-start(bf16[1024,896]{1,0:T(8,128)(2,1)} %up_ref.1) | copy-start | bytes 5505028
  98.2 41.5 %copy-start.5 = (bf16[128,1024]{1,0:T(8,128)(2,1)S(1)}, bf16[128,1024]{1,0:T(8,128)(2,1)}, u32[]{:S(2)}) copy-start(bf16[128,1024]{1,0:T(8,128)(2,1)} %pool_ref.2) | copy-start | bytes 786436
  98.2 22.2 %all-to-all-start.4 = ((bf16[32,8,512]{2,1,0:T(8,128)(2,1)}), bf16[32,8,512]{2,1,0:T(8,128)(2,1)S(1)}, u32[]{:S(2)}, u32[]{:S(2)}) async-start(bf16[32,8,512]{2,1,0:T(8,128)(2,1)} %get-tuple-element.41), calls=%async_computation.4 | async-start | bytes 524288 | tf_op jit(solution)/shard_map/all_to_all | solution.py:23
  107.3 13.1 %collective-permute-start.1 = (bf16[16,128]{1,0:T(8,128)(2,1)S(1)}, bf16[16,128]{1,0:T(8,128)(2,1)S(1)}, u32[]{:S(2)}, u32[]{:S(2)}) collective-permute-start(bf16[16,128]{1,0:T(8,128)(2,1)S(1)} %get-tuple-element.42), channel_id=1, source_target_pairs={{0,2},{2,0},{1,3},{3,1},{4,6},{6,4},{5,7},{7,5},{8,10},{10,8},{9,1... | collective-permute-start | bytes 12296 | tf_op jit(solution)/shard_map/ppermute | solution.py:389
  121.7 18.0 %all-to-all-start.5 = ((bf16[32,8,768]{2,1,0:T(8,128)(2,1)}), bf16[32,8,768]{2,1,0:T(8,128)(2,1)S(1)}, u32[]{:S(2)}, u32[]{:S(2)}) async-start(bf16[32,8,768]{2,1,0:T(8,128)(2,1)} %shard_map.79), calls=%async_computation.5 | async-start | bytes 786432 | tf_op jit(solution)/shard_map/all_to_all | solution.py:23
  139.7 31.9 %copy-start.3 = (bf16[896,1024]{1,0:T(8,128)(2,1)S(1)}, bf16[896,1024]{1,0:T(8,128)(2,1)}, u32[]{:S(2)}) copy-start(bf16[896,1024]{1,0:T(8,128)(2,1)} %down_hbm.3) | copy-start | bytes 5505028
